TPU v7x, 32 devices: a whole 2x2x4 slice. The times are simulated.
32 devices in a mesh: gx: 4 (over z), gy: 2 (over y), gz: 4 (over x, core).
Axes of the slice: x: 2, y: 2, z: 4, core: 2. Of those that a mesh axis runs over, the one named last changes fastest.
Arguments:
- cell_counts: int32 [16, 4, 16], P('gx', 'gy', 'gz'), may hold values from 64 to 128
- grid_offset: int32 [16, 4, 16, 3, 128], P('gx', 'gy', 'gz'), may hold values from 0 to 14
- fraction: float32 [16, 4, 16, 3, 128], P('gx', 'gy', 'gz'), may hold values from 0 to 1
- species: int32 [16, 4, 16, 128], P('gx', 'gy', 'gz'), may hold values from 0 to 1
- species_density: float32 [2], replicated, may hold values from 0.01 to 0.03
- species_pair: float32 [2], replicated, may hold values from 0.05 to 0.2
- species_embed: float32 [2], replicated, may hold values from 0.5 to 2
- species_charge: float32 [2], replicated, may hold values from -3 to 3
Outputs:
- forces: float32 [16, 4, 16, 3, 128], P('gx', 'gy', 'gz')
- density: float32 [16, 4, 16, 128], P('gx', 'gy', 'gz')
Inputs may be any that keep to these rules, and one draw needn't show every extreme that they name: `cell_counts`: slots below the count hold atoms; the others are padding. `grid_offset`: an atom's stencil points lie in its own cell.
All inputs are finite; a program needn't handle non-finite values.
Results may differ from a plain program's by a relative error of at most 0.0003.
Values sent between devices are 32-bit elements; how exact they have to be, the bound alone decides.
A program may use at most 128 MiB of HBM per device.

v0:
```python
import math

import jax
import jax.numpy as jnp
from jax import lax
from jax.sharding import PartitionSpec as P

NSPEC = 2
PPC = 16


EWALD_SPLIT = 0.7
COUPLING = 8.0
HIGHEST_PRECISION = lax.Precision.HIGHEST
neighbour_shifts = [
    (shift_x, shift_y, shift_z)
    for shift_x in (-1, 0, 1)
    for shift_y in (-1, 0, 1)
    for shift_z in (-1, 0, 1)
]


def padded(block, sides, width):
    for axis, dim in sides:
        count = lax.axis_size(axis)
        forward = [(i, i + 1) for i in range(count - 1)]
        forward.append((count - 1, 0))
        backward = [(target, source) for source, target in forward]
        low = lax.ppermute(
            lax.slice_in_dim(block, block.shape[dim] - width, None, axis=dim), axis, forward
        )
        high = lax.ppermute(lax.slice_in_dim(block, 0, width, axis=dim), axis, backward)
        block = jnp.concatenate([low, block, high], axis=dim)
    return block


def species_value(species, lookup_table):
    result = jnp.zeros(species.shape, jnp.float32)
    for kind_index in range(NSPEC):
        result = result + jnp.where(species == kind_index, lookup_table[kind_index], 0.0)
    return result


def stencil(offsets, fractions):
    points = lax.broadcasted_iota(jnp.int32, offsets.shape + (PPC,), offsets.ndim)
    lower_point = (points == offsets[..., None]).astype(jnp.float32)
    upper_point = (points == offsets[..., None] + 1).astype(jnp.float32)
    weights = lower_point * (1.0 - fractions[..., None]) + upper_point * fractions[..., None]
    return (weights, upper_point - lower_point)


def spread_cells(charges, weights_x, weights_y, weights_z):
    batch_size, slot_count = charges.shape
    pair_plane = (weights_y[:, :, :, None] * weights_z[:, :, None, :]).reshape(
        batch_size, slot_count, PPC * PPC
    )
    return jnp.einsum(
        "bax,bay->bxy", weights_x * charges[:, :, None], pair_plane, precision=HIGHEST_PRECISION
    )


def outer_plane(first_weights, second_weights):
    batch_size, slot_count, width_count = first_weights.shape
    return (first_weights[:, :, :, None] * second_weights[:, :, None, :]).reshape(
        batch_size, slot_count, width_count * width_count
    )


def sample_cells(blocks, charges, weights_x, weights_y, weights_z, slope_x, slope_y, slope_z):
    plain_x = jnp.einsum("bax,bxy->bay", weights_x, blocks, precision=HIGHEST_PRECISION)
    tilted_x = jnp.einsum("bax,bxy->bay", slope_x, blocks, precision=HIGHEST_PRECISION)
    force_x = -charges * jnp.sum(tilted_x * outer_plane(weights_y, weights_z), axis=2)
    force_y = -charges * jnp.sum(plain_x * outer_plane(slope_y, weights_z), axis=2)
    force_z = -charges * jnp.sum(plain_x * outer_plane(weights_y, slope_z), axis=2)
    return jnp.stack([force_x, force_y, force_z], axis=1)


def signed_modes(indices, total):
    return jnp.where(2 * indices >= total, indices - total, indices)


def green_factor(modes_x, modes_y, modes_z, length_x, length_y, length_z):
    wave_x = modes_x.astype(jnp.float32) * (2.0 * math.pi / length_x)
    wave_y = modes_y.astype(jnp.float32) * (2.0 * math.pi / length_y)
    wave_z = modes_z.astype(jnp.float32) * (2.0 * math.pi / length_z)
    squared = wave_x * wave_x + wave_y * wave_y + wave_z * wave_z
    anchor = (modes_x == 0) & (modes_y == 0) & (modes_z == 0)
    safe_square = jnp.where(anchor, 1.0, squared)
    return jnp.where(
        anchor,
        0.0,
        4.0 * math.pi * jnp.exp(-squared / (4.0 * EWALD_SPLIT * EWALD_SPLIT)) / safe_square,
    )


def dft_tables(length):
    product = lax.broadcasted_iota(jnp.int32, (length, length), 0) * lax.broadcasted_iota(
        jnp.int32, (length, length), 1
    )
    phases = (product % length).astype(jnp.float32) * (2.0 * math.pi / length)
    return (jnp.cos(phases), jnp.sin(phases))


def line_transform(real_part, imag_part, along_axis, sign_value):
    cosine_table, sine_table = dft_tables(real_part.shape[along_axis])
    real_last = jnp.moveaxis(real_part, along_axis, -1)
    imag_last = jnp.moveaxis(imag_part, along_axis, -1)
    real_cos = jnp.matmul(real_last, cosine_table, precision=HIGHEST_PRECISION)
    real_sin = jnp.matmul(real_last, sine_table, precision=HIGHEST_PRECISION)
    imag_cos = jnp.matmul(imag_last, cosine_table, precision=HIGHEST_PRECISION)
    imag_sin = jnp.matmul(imag_last, sine_table, precision=HIGHEST_PRECISION)
    new_real = real_cos - sign_value * imag_sin
    new_imag = imag_cos + sign_value * real_sin
    return (jnp.moveaxis(new_real, -1, along_axis), jnp.moveaxis(new_imag, -1, along_axis))


def pair_terms(positions, other_positions, shift_triple, not_self):
    shift_vector = jnp.asarray(shift_triple, jnp.float32)
    separation = (
        shift_vector[:, None, None] + other_positions[..., :, None, :] - positions[..., :, :, None]
    )
    squared = jnp.sum(separation * separation, axis=-3)
    weight = jnp.maximum(1.0 - squared, 0.0)
    if shift_triple == (0, 0, 0):
        weight = weight * not_self
    return (separation, weight)


def window(rows, shift_triple, cells_y, cells_z):
    return rows[
        1 + shift_triple[0],
        1 + shift_triple[1] : 1 + shift_triple[1] + cells_y,
        1 + shift_triple[2] : 1 + shift_triple[2] + cells_z,
    ]


def on_device(
    cell_counts,
    grid_offset,
    fraction,
    species,
    species_density,
    species_pair,
    species_embed,
    species_charge,
):
    cells_x, cells_y, cells_z, components, slot_count = fraction.shape
    slot_index = lax.broadcasted_iota(jnp.int32, species.shape, 3)
    alive_mask = (slot_index < cell_counts[..., None]).astype(jnp.float32)
    positions = (grid_offset.astype(jnp.float32) + 0.5 + fraction) / PPC
    density_coef = species_value(species, species_density) * alive_mask
    repulsion = species_value(species, species_pair) * alive_mask
    embedding = species_value(species, species_embed)
    charge = species_value(species, species_charge) * alive_mask
    not_self = (
        lax.broadcasted_iota(jnp.int32, (slot_count, slot_count), 0)
        != lax.broadcasted_iota(jnp.int32, (slot_count, slot_count), 1)
    ).astype(jnp.float32)
    packed_atoms = jnp.concatenate(
        [positions, density_coef[:, :, :, None, :], repulsion[:, :, :, None, :]], axis=3
    )
    extended = padded(packed_atoms, (("gx", 0), ("gy", 1), ("gz", 2)), 1)
    row_ids = jnp.arange(cells_x, dtype=jnp.int32)

    def density_row(row):
        near_rows = lax.dynamic_slice_in_dim(extended, row, 3, 0)
        own = lax.dynamic_index_in_dim(positions, row, 0, keepdims=False)
        total = jnp.zeros((cells_y, cells_z, slot_count), jnp.float32)
        for shift_triple in neighbour_shifts:
            near = window(near_rows, shift_triple, cells_y, cells_z)
            separation, weight = pair_terms(own, near[:, :, 0:3, :], shift_triple, not_self)
            total = total + jnp.sum(
                weight * weight * weight * near[:, :, 3, :][..., None, :], axis=-1
            )
        return total

    density = lax.map(density_row, row_ids) * alive_mask
    slope_embed = -embedding * alive_mask / (2.0 * jnp.sqrt(1.0 + density))
    extended_slope = padded(slope_embed, (("gx", 0), ("gy", 1), ("gz", 2)), 1)

    def force_row(row):
        near_rows = lax.dynamic_slice_in_dim(extended, row, 3, 0)
        near_slopes = lax.dynamic_slice_in_dim(extended_slope, row, 3, 0)
        own = lax.dynamic_index_in_dim(positions, row, 0, keepdims=False)
        own_rep = lax.dynamic_index_in_dim(repulsion, row, 0, keepdims=False)
        own_coef = lax.dynamic_index_in_dim(density_coef, row, 0, keepdims=False)
        own_slope = lax.dynamic_index_in_dim(slope_embed, row, 0, keepdims=False)
        total = jnp.zeros((cells_y, cells_z, 3, slot_count), jnp.float32)
        for shift_triple in neighbour_shifts:
            near = window(near_rows, shift_triple, cells_y, cells_z)
            separation, weight = pair_terms(own, near[:, :, 0:3, :], shift_triple, not_self)
            other_coef = near[:, :, 3, :][..., None, :]
            other_rep = near[:, :, 4, :][..., None, :]
            other_slope = window(near_slopes, shift_triple, cells_y, cells_z)[..., None, :]
            coefficient = -2.0 * own_rep[
                ..., :, None
            ] * other_rep * weight - 3.0 * weight * weight * (
                own_slope[..., :, None] * other_coef + other_slope * own_coef[..., :, None]
            )
            total = total + 2.0 * jnp.sum(coefficient[..., None, :, :] * separation, axis=-1)
        return total

    eam_force = lax.map(force_row, row_ids)
    flat_cells = cells_x * cells_y * cells_z

    def flatten(values):
        return values.reshape((flat_cells,) + values.shape[3:])

    stencils = [
        stencil(
            flatten(grid_offset[:, :, :, axis_index, :]), flatten(fraction[:, :, :, axis_index, :])
        )
        for axis_index in range(3)
    ]
    flat_charge = flatten(charge)
    blocks = spread_cells(flat_charge, stencils[0][0], stencils[1][0], stencils[2][0])
    charge_brick = (
        blocks.reshape(cells_x, cells_y, cells_z, PPC, PPC, PPC)
        .transpose(0, 3, 1, 4, 2, 5)
        .reshape(cells_x * PPC, cells_y * PPC, cells_z * PPC)
    )
    brick_x, brick_y, brick_z = charge_brick.shape
    length_x = brick_x * lax.axis_size("gx")
    length_y = brick_y * lax.axis_size("gy")
    depth_lines = lax.all_to_all(charge_brick, "gz", split_axis=1, concat_axis=2, tiled=True)
    quarter_y = depth_lines.shape[1]
    depth_length = depth_lines.shape[2]
    cosine_table, sine_table = dft_tables(depth_length)
    line_real = jnp.matmul(depth_lines, cosine_table, precision=HIGHEST_PRECISION)
    line_imag = -jnp.matmul(depth_lines, sine_table, precision=HIGHEST_PRECISION)
    stacked = jnp.stack([line_real, line_imag])[:, None]
    planes = lax.all_to_all(stacked, ("gx", "gy", "gz"), split_axis=4, concat_axis=1, tiled=True)
    group_size = planes.shape[1]
    rows_gx = lax.axis_size("gx")
    rest_count = group_size // rows_gx
    plane_depth = planes.shape[4]
    planes = (
        planes.reshape(2, rows_gx, rest_count, brick_x, quarter_y, plane_depth)
        .transpose(0, 5, 1, 3, 2, 4)
        .reshape(2, plane_depth, length_x, length_y)
    )
    real_part, imag_part = line_transform(planes[0], planes[1], 2, -1.0)
    real_part, imag_part = line_transform(real_part, imag_part, 1, -1.0)
    first_mode = lax.axis_index(("gx", "gy", "gz")) * plane_depth
    modes_z = signed_modes(
        first_mode + lax.broadcasted_iota(jnp.int32, (plane_depth, 1, 1), 0), depth_length
    )
    modes_x = signed_modes(lax.broadcasted_iota(jnp.int32, (1, length_x, 1), 1), length_x)
    modes_y = signed_modes(lax.broadcasted_iota(jnp.int32, (1, 1, length_y), 2), length_y)
    factor = green_factor(modes_x, modes_y, modes_z, length_x, length_y, depth_length)
    real_part, imag_part = line_transform(real_part * factor, imag_part * factor, 1, 1.0)
    real_part, imag_part = line_transform(real_part, imag_part, 2, 1.0)
    planes_return = (
        jnp.stack([real_part, imag_part])
        .reshape(2, plane_depth, rows_gx, brick_x, rest_count, quarter_y)
        .transpose(0, 2, 4, 3, 5, 1)
        .reshape(2, group_size, brick_x, quarter_y, plane_depth)
    )
    returned = lax.all_to_all(
        planes_return, ("gx", "gy", "gz"), split_axis=1, concat_axis=4, tiled=True
    )
    real_part, imag_part = (returned[0, 0], returned[1, 0])
    potential_lines = (
        jnp.matmul(real_part, cosine_table, precision=HIGHEST_PRECISION)
        - jnp.matmul(imag_part, sine_table, precision=HIGHEST_PRECISION)
    ) / (length_x * length_y * depth_length)
    potential = lax.all_to_all(potential_lines, "gz", split_axis=2, concat_axis=1, tiled=True)
    blocks_back = (
        potential.reshape(cells_x, PPC, cells_y, PPC, cells_z, PPC)
        .transpose(0, 2, 4, 1, 3, 5)
        .reshape(flat_cells, PPC, PPC * PPC)
    )
    electric = sample_cells(
        blocks_back,
        flat_charge,
        stencils[0][0],
        stencils[1][0],
        stencils[2][0],
        stencils[0][1],
        stencils[1][1],
        stencils[2][1],
    ).reshape(cells_x, cells_y, cells_z, 3, slot_count)
    forces = (eam_force + COUPLING * electric) * alive_mask[:, :, :, None, :]
    return (forces, density)


def solution(mesh):
    return jax.shard_map(
        on_device,
        mesh=mesh,
        in_specs=(
            P("gx", "gy", "gz"),
            P("gx", "gy", "gz", None, None),
            P("gx", "gy", "gz", None, None),
            P("gx", "gy", "gz", None),
            P(),
            P(),
            P(),
            P(),
        ),
        out_specs=(P("gx", "gy", "gz", None, None), P("gx", "gy", "gz", None)),
        check_vma=False,
    )
```

profile of v0, /device:TPU:1, one launch (start us, length us, event | category | flops | bytes accessed | tf_op | source)
XLA Modules:
  0.0 467.6 jit_solution(6046106370680554486)
XLA Ops:
  3.7 4.5 broadcast_multiply_fusion
  16.4 6.8 %copy.257 = f32[4,2,4,16,16,16]{5,2,4,1,3,0:T(4,128)} copy(f32[4,2,4,16,16,16]{5,4,3,2,1,0:T(8,128)} %reshape.1344) | data formatting | bytes 1048576 | tf_op jit(solution)/shard_map/reshape | solution.py:218
  28.3 12.0 %all_to_all.63 = f32[4,1,32768]{2,1,0:T(1,128)S(1)} all-to-all(f32[4,1,32768]{2,1,0:T(1,128)S(1)} %reshape.1380), channel_id=1, replica_groups=mesh['gx'=4,'gy'=2,'gz'=4] {'gz'}, dimensions={0} | all-to-all | bytes 1048576 | tf_op jit(solution)/shard_map/all_to_all | solution.py:225
  53.9 5.7 %all-to-all-start.1 = ((f32[32,1,8192]{2,1,0:T(1,128)}), f32[32,1,8192]{2,1,0:T(1,128)S(1)}, u32[]{:S(2)}, u32[]{:S(2)}) async-start(f32[32,1,8192]{2,1,0:T(1,128)} %reshape.1382), calls=%async_computation.1 | async-start | bytes 2097152 | tf_op jit(solution)/shard_map/all_to_all | solution.py:232
  59.9 24.9 %all-to-all-done.1 = f32[32,1,8192]{2,1,0:T(1,128)S(1)} async-done(((f32[32,1,8192]{2,1,0:T(1,128)}), f32[32,1,8192]{2,1,0:T(1,128)S(1)}, u32[]{:S(2)}, u32[]{:S(2)}) %all-to-all-start.1) | async-done | bytes 1048608 | tf_op jit(solution)/shard_map/all_to_all | solution.py:232
  122.1 4.6 all-to-all-start.2
  134.0 13.9 %collective-permute-done = f32[1,2,4,5,128]{4,3,2,1,0:T(8,128)S(1)} collective-permute-done((f32[1,2,4,5,128]{4,3,2,1,0:T(8,128)S(1)}, f32[1,2,4,5,128]{4,3,2,1,0:T(8,128)S(1)}, u32[]{:S(2)}, u32[]{:S(2)}) %collective-permute-start) | collective-permute-done | bytes 20512 | tf_op jit(solution)/shard_map/ppermute | solution.py:29
  149.7 5.6 %copy.229 = f32[32,128,256]{2,1,0:T(8,128)} copy(f32[32,128,256]{1,2,0:T(8,128)} %bitcast.763) | data formatting | bytes 8388608 | tf_op jit(solution)/shard_map/mul | solution.py:54
  155.3 5.6 %copy.230 = f32[32,128,256]{2,1,0:T(8,128)} copy(f32[32,128,256]{1,2,0:T(8,128)} %bitcast.767) | data formatting | bytes 8388608 | tf_op jit(solution)/shard_map/mul | solution.py:64
  160.9 5.6 %copy.231 = f32[32,128,256]{2,1,0:T(8,128)} copy(f32[32,128,256]{1,2,0:T(8,128)} %bitcast.766) | data formatting | bytes 8388608 | tf_op jit(solution)/shard_map/mul | solution.py:64
  192.7 87.3 %while.26 = (s32[]{:T(128)}, f32[4,2,4,128]{3,2,1,0:T(4,128)S(1)}, s32[4]{0:T(128)S(1)}, f32[6,4,6,5,128]{4,2,1,3,0:T(8,128)S(1)}, f32[4,2,4,3,128]{4,3,2,1,0:T(...) while((s32[]{:T(128)}, f32[4,2,4,128]{3,2,1,0:T(4,128)S(1)}, ...), condition=%wide.region_55.56_spmd.clone.clone.clone, body=%wide.region_0.55_spmd.sunk.clone.clone.sunk.clone | while | flops 49787912 | bytes 31814928 | solution.py:177
  200.0 5.2 %multiply_reduce_fusion.35 = (f32[2,4,128,128]{3,2,1,0:T(8,128)S(1)}, f32[2,4,128,128]{3,2,1,0:T(8,128)S(1)}, f32[2,4,128,128]{3,2,1,0:T(8,128)S(1)}, f32[2,4,12...) fusion(f32[2,4,3,128]{3,2,1,0:T(4,128)S(1)} %copy.382, ...), kind=kLoop, calls=%fused_computation.27.clone.1.clone | loop fusion | flops 18874368 | bytes 9670656 | tf_op jit(solution)/shard_map/while/body/eval_jaxpr/reduce_sum | solution.py:122
  221.8 5.2 %multiply_reduce_fusion.35 = (f32[2,4,128,128]{3,2,1,0:T(8,128)S(1)}, f32[2,4,128,128]{3,2,1,0:T(8,128)S(1)}, f32[2,4,128,128]{3,2,1,0:T(8,128)S(1)}, f32[2,4,12...) fusion(f32[2,4,3,128]{3,2,1,0:T(4,128)S(1)} %copy.382, ...), kind=kLoop, calls=%fused_computation.27.clone.1.clone | loop fusion | flops 18874368 | bytes 9670656 | tf_op jit(solution)/shard_map/while/body/eval_jaxpr/reduce_sum | solution.py:122
  243.6 5.2 %multiply_reduce_fusion.35 = (f32[2,4,128,128]{3,2,1,0:T(8,128)S(1)}, f32[2,4,128,128]{3,2,1,0:T(8,128)S(1)}, f32[2,4,128,128]{3,2,1,0:T(8,128)S(1)}, f32[2,4,12...) fusion(f32[2,4,3,128]{3,2,1,0:T(4,128)S(1)} %copy.382, ...), kind=kLoop, calls=%fused_computation.27.clone.1.clone | loop fusion | flops 18874368 | bytes 9670656 | tf_op jit(solution)/shard_map/while/body/eval_jaxpr/reduce_sum | solution.py:122
  265.4 5.2 %multiply_reduce_fusion.35 = (f32[2,4,128,128]{3,2,1,0:T(8,128)S(1)}, f32[2,4,128,128]{3,2,1,0:T(8,128)S(1)}, f32[2,4,128,128]{3,2,1,0:T(8,128)S(1)}, f32[2,4,12...) fusion(f32[2,4,3,128]{3,2,1,0:T(4,128)S(1)} %copy.382, ...), kind=kLoop, calls=%fused_computation.27.clone.1.clone | loop fusion | flops 18874368 | bytes 9670656 | tf_op jit(solution)/shard_map/while/body/eval_jaxpr/reduce_sum | solution.py:122
  286.7 4.7 copy.228
  294.9 5.8 %multiply_reduce_fusion.29 = f32[32,128]{1,0:T(8,128)S(1)} fusion(f32[32,128,256]{2,1,0:T(8,128)} %copy.229, f32[32,16,256]{2,1,0:T(8,128)S(1)} %reshape.1349, s32[32,128]{1,0:T(8,128)S(1)} %bitcast.790, s32[32,128]{1,0:T(8,128)S(1)} %broadcast_add_fusion.3), kind=kOutput, calls=%fused_computation.579 | convolution fusion | flops 203747328 | bytes 4767744 | tf_op jit(solution)/shard_map/bax,bxy->bay/dot_general | solution.py:71
  300.9 6.6 %multiply_reduce_fusion.28 = (f32[32,128]{1,0:T(8,128)S(1)}, f32[32,128]{1,0:T(8,128)S(1)}) fusion(f32[32,128,256]{2,1,0:T(8,128)S(1)} %copy-done.1, f32[32,128,256]{2,1,0:T(8,128)} %copy.231, f32[32,16,256]{2,1,0:T(8,128)S(1)} %reshape.1349, f32[32,128]{1,0:T(8,128)S(1)} %bitcast.794, f32[32,128]{1,0:T(8,128)S(1)} %broadcast_subtract_fusion.2, ...), kind=kOutput, calls=%fused_computation.578 | convolution fusion | flops 205840384 | bytes 9011200 | tf_op jit(solution)/shard_map/bax,bxy->bay/dot_general | solution.py:70
  310.7 5.3 %collective-permute-start.6 = (f32[1,2,4,128]{3,2,1,0:T(4,128)S(1)}, f32[1,2,4,128]{3,2,1,0:T(4,128)S(1)}, u32[]{:S(2)}, u32[]{:S(2)}) collective-permute-start(f32[1,2,4,128]{3,2,1,0:T(4,128)S(1)} %get-tuple-element.982), channel_id=1, source_target_pairs={{0,8},{8,16},{16,24},{24,0},{1,9},{9,17},{17,25},{25,1},{2,10},{10... | collective-permute-start | bytes 12296 | tf_op jit(solution)/shard_map/ppermute | solution.py:29
  329.1 137.6 %while.27 = (s32[]{:T(128)}, f32[4,2,4,3,128]{4,2,1,0,3:T(4,128)S(1)}, s32[4]{0:T(128)S(1)}, f32[4,2,4,128]{3,2,1,0:T(4,128)S(1)}, f32[6,4,6,5,128]{4,2,1,3,0:T(...) while((s32[]{:T(128)}, ...), condition=%wide.region_111.112_spmd.clone.clone.clone, body=%wide.region_56.111_spmd.sunk.clone.clone.sunk.clone | while | flops 99335176 | bytes 61772524 | solution.py:203
  340.1 4.6 fusion.550
  353.4 4.7 %fusion.558 = (f32[2,4,3,128]{3,2,1,0:T(4,128)S(1)}, f32[2,4,3,128]{3,2,1,0:T(4,128)S(1)}, f32[2,4,3,128]{3,2,1,0:T(4,128)S(1)}, f32[2,4,3,128]{3,2,1,0:T(4,128)...) fusion(f32[2,4,128,128]{3,2,1,0:T(8,128)S(1)} %get-tuple-elemen, ...), kind=kLoop, calls=%fused_computation.265.clone.1.clone | loop fusion | flops 10589184 | bytes 4952064 | tf_op jit(solution)/shard_map/while/body/eval_jaxpr/reduce_sum | solution.py:200
  358.9 4.7 %fusion.554 = (f32[2,4,3,128]{3,2,1,0:T(4,128)S(1)}, f32[2,4,3,128]{3,2,1,0:T(4,128)S(1)}, f32[2,4,3,128]{3,2,1,0:T(4,128)S(1)}, f32[2,4,3,128]{3,2,1,0:T(4,128)...) fusion(f32[2,4,128,128]{3,2,1,0:T(8,128)S(1)} %get-tuple-elemen, ...), kind=kLoop, calls=%fused_computation.263.clone.1.clone | loop fusion | flops 10589184 | bytes 4952064 | tf_op jit(solution)/shard_map/while/body/eval_jaxpr/reduce_sum | solution.py:200
  374.4 4.6 fusion.550
  387.7 4.7 %fusion.558 = (f32[2,4,3,128]{3,2,1,0:T(4,128)S(1)}, f32[2,4,3,128]{3,2,1,0:T(4,128)S(1)}, f32[2,4,3,128]{3,2,1,0:T(4,128)S(1)}, f32[2,4,3,128]{3,2,1,0:T(4,128)...) fusion(f32[2,4,128,128]{3,2,1,0:T(8,128)S(1)} %get-tuple-elemen, ...), kind=kLoop, calls=%fused_computation.265.clone.1.clone | loop fusion | flops 10589184 | bytes 4952064 | tf_op jit(solution)/shard_map/while/body/eval_jaxpr/reduce_sum | solution.py:200
  393.2 4.7 %fusion.554 = (f32[2,4,3,128]{3,2,1,0:T(4,128)S(1)}, f32[2,4,3,128]{3,2,1,0:T(4,128)S(1)}, f32[2,4,3,128]{3,2,1,0:T(4,128)S(1)}, f32[2,4,3,128]{3,2,1,0:T(4,128)...) fusion(f32[2,4,128,128]{3,2,1,0:T(8,128)S(1)} %get-tuple-elemen, ...), kind=kLoop, calls=%fused_computation.263.clone.1.clone | loop fusion | flops 10589184 | bytes 4952064 | tf_op jit(solution)/shard_map/while/body/eval_jaxpr/reduce_sum | solution.py:200
  408.7 4.6 fusion.550
  422.1 4.7 %fusion.558 = (f32[2,4,3,128]{3,2,1,0:T(4,128)S(1)}, f32[2,4,3,128]{3,2,1,0:T(4,128)S(1)}, f32[2,4,3,128]{3,2,1,0:T(4,128)S(1)}, f32[2,4,3,128]{3,2,1,0:T(4,128)...) fusion(f32[2,4,128,128]{3,2,1,0:T(8,128)S(1)} %get-tuple-elemen, ...), kind=kLoop, calls=%fused_computation.265.clone.1.clone | loop fusion | flops 10589184 | bytes 4952064 | tf_op jit(solution)/shard_map/while/body/eval_jaxpr/reduce_sum | solution.py:200
  427.5 4.7 %fusion.554 = (f32[2,4,3,128]{3,2,1,0:T(4,128)S(1)}, f32[2,4,3,128]{3,2,1,0:T(4,128)S(1)}, f32[2,4,3,128]{3,2,1,0:T(4,128)S(1)}, f32[2,4,3,128]{3,2,1,0:T(4,128)...) fusion(f32[2,4,128,128]{3,2,1,0:T(8,128)S(1)} %get-tuple-elemen, ...), kind=kLoop, calls=%fused_computation.263.clone.1.clone | loop fusion | flops 10589184 | bytes 4952064 | tf_op jit(solution)/shard_map/while/body/eval_jaxpr/reduce_sum | solution.py:200
  443.1 4.6 fusion.550
  456.4 4.7 %fusion.558 = (f32[2,4,3,128]{3,2,1,0:T(4,128)S(1)}, f32[2,4,3,128]{3,2,1,0:T(4,128)S(1)}, f32[2,4,3,128]{3,2,1,0:T(4,128)S(1)}, f32[2,4,3,128]{3,2,1,0:T(4,128)...) fusion(f32[2,4,128,128]{3,2,1,0:T(8,128)S(1)} %get-tuple-elemen, ...), kind=kLoop, calls=%fused_computation.265.clone.1.clone | loop fusion | flops 10589184 | bytes 4952064 | tf_op jit(solution)/shard_map/while/body/eval_jaxpr/reduce_sum | solution.py:200
  461.9 4.7 %fusion.554 = (f32[2,4,3,128]{3,2,1,0:T(4,128)S(1)}, f32[2,4,3,128]{3,2,1,0:T(4,128)S(1)}, f32[2,4,3,128]{3,2,1,0:T(4,128)S(1)}, f32[2,4,3,128]{3,2,1,0:T(4,128)...) fusion(f32[2,4,128,128]{3,2,1,0:T(8,128)S(1)} %get-tuple-elemen, ...), kind=kLoop, calls=%fused_computation.263.clone.1.clone | loop fusion | flops 10589184 | bytes 4952064 | tf_op jit(solution)/shard_map/while/body/eval_jaxpr/reduce_sum | solution.py:200
  (909 shorter events, 248.2 us)
Async XLA Ops:
  53.9 30.9 %all-to-all-start.1 = ((f32[32,1,8192]{2,1,0:T(1,128)}), f32[32,1,8192]{2,1,0:T(1,128)S(1)}, u32[]{:S(2)}, u32[]{:S(2)}) async-start(f32[32,1,8192]{2,1,0:T(1,128)} %reshape.1382), calls=%async_computation.1 | async-start | bytes 2097152 | tf_op jit(solution)/shard_map/all_to_all | solution.py:232
  122.1 51.9 %all-to-all-start.2 = ((f32[32,1,8192]{2,1,0:T(1,128)}), f32[32,1,8192]{2,1,0:T(1,128)S(1)}, u32[]{:S(2)}, u32[]{:S(2)}) async-start(f32[32,1,8192]{2,1,0:T(1,128)} %reshape.1384), calls=%async_computation.2 | async-start | bytes 2097152 | tf_op jit(solution)/shard_map/all_to_all | solution.py:259
  130.7 17.2 %collective-permute-start = (f32[1,2,4,5,128]{4,3,2,1,0:T(8,128)S(1)}, f32[1,2,4,5,128]{4,3,2,1,0:T(8,128)S(1)}, u32[]{:S(2)}, u32[]{:S(2)}) collective-permute-start(f32[1,2,4,5,128]{4,3,2,1,0:T(8,128)S(1)} %get-tuple-element.966), channel_id=1, source_target_pairs={{0,8},{8,16},{16,24},{24,0},{1,9},{9,17},{17,25},{25,1},{2,10},{10... | collective-permute-start | bytes 61448 | tf_op jit(solution)/shard_map/ppermute | solution.py:29
  132.1 15.8 %collective-permute-start.1 = (f32[1,2,4,5,128]{4,3,2,1,0:T(8,128)S(1)}, f32[1,2,4,5,128]{4,3,2,1,0:T(8,128)S(1)}, u32[]{:S(2)}, u32[]{:S(2)}) collective-permute-start(f32[1,2,4,5,128]{4,3,2,1,0:T(8,128)S(1)} %get-tuple-element.967), channel_id=1, source_target_pairs={{8,0},{16,8},{24,16},{0,24},{9,1},{17,9},{25,17},{1,25},{10,2},{18... | collective-permute-start | bytes 61448 | tf_op jit(solution)/shard_map/ppermute | solution.py:32
  148.0 18.5 %collective-permute-start.2 = (f32[6,1,4,5,128]{4,3,2,1,0:T(8,128)S(1)}, f32[6,1,4,5,128]{4,3,2,1,0:T(8,128)S(1)}, u32[]{:S(2)}, u32[]{:S(2)}) collective-permute-start(f32[6,1,4,5,128]{4,3,2,1,0:T(8,128)S(1)} %get-tuple-element.964), channel_id=1, source_target_pairs={{0,4},{4,0},{1,5},{5,1},{2,6},{6,2},{3,7},{7,3},{8,12},{12,8},{9,1... | collective-permute-start | bytes 184328 | tf_op jit(solution)/shard_map/ppermute | solution.py:29
  149.6 16.9 %collective-permute-start.3 = (f32[6,1,4,5,128]{4,3,2,1,0:T(8,128)S(1)}, f32[6,1,4,5,128]{4,3,2,1,0:T(8,128)S(1)}, u32[]{:S(2)}, u32[]{:S(2)}) collective-permute-start(f32[6,1,4,5,128]{4,3,2,1,0:T(8,128)S(1)} %get-tuple-element.965), channel_id=1, source_target_pairs={{4,0},{0,4},{5,1},{1,5},{6,2},{2,6},{7,3},{3,7},{12,8},{8,12},{13,... | collective-permute-start | bytes 184328 | tf_op jit(solution)/shard_map/ppermute | solution.py:32
  160.9 8.9 %copy-start.41 = (f32[2]{0:T(128)S(1)}, f32[2]{0:T(128)}, u32[]{:S(2)}) copy-start(f32[2]{0:T(128)} %param.72) | copy-start | bytes 28
  166.6 5.0 %collective-permute-start.4 = (f32[6,4,1,5,128]{4,3,2,1,0:T(8,128)S(1)}, f32[6,4,1,5,128]{4,3,2,1,0:T(8,128)S(1)}, u32[]{:S(2)}, u32[]{:S(2)}) collective-permute-start(f32[6,4,1,5,128]{4,3,2,1,0:T(8,128)S(1)} %get-tuple-element.959), channel_id=1, source_target_pairs={{0,1},{1,2},{2,3},{3,0},{4,5},{5,6},{6,7},{7,4},{8,9},{9,10},{10,1... | collective-permute-start | bytes 184328 | tf_op jit(solution)/shard_map/ppermute | solution.py:29
  169.7 4.0 collective-permute-start.5
  188.7 91.2 %all-to-all-start.3 = ((f32[4,1,32768]{2,1,0:T(1,128)}), f32[4,1,32768]{2,1,0:T(1,128)S(1)}, u32[]{:S(2)}, u32[]{:S(2)}) async-start(f32[4,1,32768]{2,1,0:T(1,128)} %reshape.1386), calls=%async_computation.3 | async-start | bytes 1048576 | tf_op jit(solution)/shard_map/all_to_all | solution.py:267
  300.7 28.2 %copy-start.7 = (f32[3]{0:T(128)S(1)}, f32[3]{0:T(128)}, u32[]{:S(2)}) copy-start(f32[3]{0:T(128)} %get-tuple-element.2445) | copy-start | bytes 40
  300.7 28.2 %copy-start.8 = (f32[3]{0:T(128)S(1)}, f32[3]{0:T(128)}, u32[]{:S(2)}) copy-start(f32[3]{0:T(128)} %get-tuple-element.2446) | copy-start | bytes 40
  300.7 28.2 %copy-start.9 = (f32[3]{0:T(128)S(1)}, f32[3]{0:T(128)}, u32[]{:S(2)}) copy-start(f32[3]{0:T(128)} %get-tuple-element.2447) | copy-start | bytes 40
  300.7 28.2 %copy-start.10 = (f32[3]{0:T(128)S(1)}, f32[3]{0:T(128)}, u32[]{:S(2)}) copy-start(f32[3]{0:T(128)} %get-tuple-element.2448) | copy-start | bytes 40
  300.8 28.2 %copy-start.11 = (f32[3]{0:T(128)S(1)}, f32[3]{0:T(128)}, u32[]{:S(2)}) copy-start(f32[3]{0:T(128)} %get-tuple-element.2449) | copy-start | bytes 40
  300.8 28.2 %copy-start.12 = (f32[3]{0:T(128)S(1)}, f32[3]{0:T(128)}, u32[]{:S(2)}) copy-start(f32[3]{0:T(128)} %get-tuple-element.2450) | copy-start | bytes 40
  300.8 28.2 %copy-start.13 = (f32[3]{0:T(128)S(1)}, f32[3]{0:T(128)}, u32[]{:S(2)}) copy-start(f32[3]{0:T(128)} %get-tuple-element.2451) | copy-start | bytes 40
  300.8 28.2 %copy-start.14 = (f32[3]{0:T(128)S(1)}, f32[3]{0:T(128)}, u32[]{:S(2)}) copy-start(f32[3]{0:T(128)} %get-tuple-element.2452) | copy-start | bytes 40
  300.8 28.2 %copy-start.16 = (f32[3]{0:T(128)S(1)}, f32[3]{0:T(128)}, u32[]{:S(2)}) copy-start(f32[3]{0:T(128)} %get-tuple-element.2453) | copy-start | bytes 40
  300.8 28.2 %copy-start.18 = (f32[3]{0:T(128)S(1)}, f32[3]{0:T(128)}, u32[]{:S(2)}) copy-start(f32[3]{0:T(128)} %get-tuple-element.2454) | copy-start | bytes 40
  300.8 28.2 %copy-start.20 = (f32[3]{0:T(128)S(1)}, f32[3]{0:T(128)}, u32[]{:S(2)}) copy-start(f32[3]{0:T(128)} %get-tuple-element.2455) | copy-start | bytes 40
  300.8 28.2 %copy-start.22 = (f32[3]{0:T(128)S(1)}, f32[3]{0:T(128)}, u32[]{:S(2)}) copy-start(f32[3]{0:T(128)} %get-tuple-element.2456) | copy-start | bytes 40
  300.9 28.2 %copy-start.24 = (f32[3]{0:T(128)S(1)}, f32[3]{0:T(128)}, u32[]{:S(2)}) copy-start(f32[3]{0:T(128)} %get-tuple-element.2457) | copy-start | bytes 40
  300.9 28.2 %copy-start.26 = (f32[3]{0:T(128)S(1)}, f32[3]{0:T(128)}, u32[]{:S(2)}) copy-start(f32[3]{0:T(128)} %get-tuple-element.2458) | copy-start | bytes 40
  300.9 28.2 %copy-start.28 = (f32[3]{0:T(128)S(1)}, f32[3]{0:T(128)}, u32[]{:S(2)}) copy-start(f32[3]{0:T(128)} %get-tuple-element.2459) | copy-start | bytes 40
  300.9 28.2 %copy-start.30 = (f32[3]{0:T(128)S(1)}, f32[3]{0:T(128)}, u32[]{:S(2)}) copy-start(f32[3]{0:T(128)} %get-tuple-element.2460) | copy-start | bytes 40
  310.7 6.0 %collective-permute-start.6 = (f32[1,2,4,128]{3,2,1,0:T(4,128)S(1)}, f32[1,2,4,128]{3,2,1,0:T(4,128)S(1)}, u32[]{:S(2)}, u32[]{:S(2)}) collective-permute-start(f32[1,2,4,128]{3,2,1,0:T(4,128)S(1)} %get-tuple-element.982), channel_id=1, source_target_pairs={{0,8},{8,16},{16,24},{24,0},{1,9},{9,17},{17,25},{25,1},{2,10},{10... | collective-permute-start | bytes 12296 | tf_op jit(solution)/shard_map/ppermute | solution.py:29
  316.0 2.5 collective-permute-start.7
  318.4 2.6 collective-permute-start.8
  319.7 2.5 collective-permute-start.9
  322.3 4.3 collective-permute-start.10
  325.8 3.1 collective-permute-start.11
  (49 other events, 274.1 us)
where the time goes:
time: 477 us; the launch traced here: 468 us
  other arithmetic  213 us (45%)
  local copies, waits for them, and re-layouts  85.4 us (18%)
  waiting for transfers between devices  50 us (10%)
  matrix products  43 us (9%)
  starting transfers between devices  32.7 us (7%)
  loops' own time  29.1 us (6%)
  blocking collectives  12 us (3%)
    reduce_sum x16, other arithmetic, force_row(): jnp.sum(coefficient[..., None, :, :] * separation, axis=-1)  71.3 us
    reduce_sum x16, other arithmetic, pair_terms(): squared = jnp.sum(separation * separation, axis=-3)  44.5 us
    sub x32, other arithmetic, force_row(): -2.0 * own_rep[..., :, None] * other_rep * weight  27.6 us
    all_to_all x1, waiting for transfers between devices, on_device(): lax.all_to_all(stacked, ('gx', 'gy', 'gz'), split_axis=4, concat_axis=1,...  24.9 us
    reduce_sum x108, other arithmetic, density_row(): jnp.sum(weight * weight * weight * near[:, :, 3, :][..., None, :], axis=-1)  23.8 us
    add x104, other arithmetic, pair_terms(): shift_vector[:, None, None] + other_positions[..., :, None, :]  18.6 us
    ppermute x6, waiting for transfers between devices, padded(): lax.ppermute(lax.slice_in_dim(block, block.shape[dim] - width, None, axis...  17.6 us
    ppermute x6, starting transfers between devices, padded(): lax.ppermute(lax.slice_in_dim(block, block.shape[dim] - width, None, axis...  16.2 us
  transfers between devices with their start and end apart: 15, of which 10 were waited for; matrix products, arithmetic and copies ran while one was open for 20% of the time, Pallas kernels for 0%

commit v1 on v0

v1 whole, which is shorter than its diff:
```python
import math

import jax
import jax.numpy as jnp
import numpy as np
from jax import lax
from jax.experimental import pallas as pl
from jax.experimental.pallas import tpu as pltpu
from jax.sharding import PartitionSpec as P

PPC = 16
EWALD_SPLIT = 0.7
COUPLING = 8.0
KF = 32
NT = (((1,), (1,)), ((), ()))
NN = (((1,), (0,)), ((), ()))
VM = pl.BlockSpec(memory_space=pltpu.VMEM)
SM = pl.BlockSpec(memory_space=pltpu.SMEM)


def padded(block, sides, widths):
    for (axis, dim), width in zip(sides, widths):
        count = lax.axis_size(axis)
        forward = [(i, (i + 1) % count) for i in range(count)]
        backward = [(target, source) for source, target in forward]
        low = lax.ppermute(
            lax.slice_in_dim(block, block.shape[dim] - width, None, axis=dim), axis, forward
        )
        high = lax.ppermute(lax.slice_in_dim(block, 0, width, axis=dim), axis, backward)
        block = jnp.concatenate([low, block, high], axis=dim)
    return block


def split2(values):
    high = values.astype(jnp.bfloat16)
    low = (values - high.astype(jnp.float32)).astype(jnp.bfloat16)
    return high, low


def split3(values):
    high = values.astype(jnp.bfloat16).astype(jnp.float32)
    rest = values - high
    mid = rest.astype(jnp.bfloat16).astype(jnp.float32)
    low = (rest - mid).astype(jnp.bfloat16).astype(jnp.float32)
    return high, mid, low


def mm(a, b, dims=NN):
    return lax.dot_general(a, b, dims, preferred_element_type=jnp.float32)


def mm3(a, b, dims=NN):
    return mm(a[0], b[0], dims) + mm(a[0], b[1], dims) + mm(a[1], b[0], dims)


def table(sp, ref):
    result = jnp.zeros(sp.shape, jnp.float32)
    for kind in range(ref.shape[0]):
        result = jnp.where(sp == kind, ref[kind], result)
    return result


def weights_of(off, fr):
    points = lax.broadcasted_iota(jnp.int32, (PPC, off.shape[1]), 0)
    lower = points == off
    upper = points == off + 1
    zero = jnp.zeros((PPC, off.shape[1]), jnp.float32)
    weights = jnp.where(lower, 1.0 - fr, jnp.where(upper, fr, zero))
    slopes = jnp.where(lower, -1.0, jnp.where(upper, 1.0, zero))
    return weights, slopes


def placed(rows, cell, cells):
    parts = []
    if cell:
        parts.append(jnp.zeros((cell * PPC, rows.shape[1]), jnp.float32))
    parts.append(rows)
    if cell < cells - 1:
        parts.append(jnp.zeros(((cells - 1 - cell) * PPC, rows.shape[1]), jnp.float32))
    return jnp.concatenate(parts, axis=0)


def spread_kernel(cnt, off, fr, sp, tden, tpair, temb, tchg, s_ref, pk_ref):
    nx, ny, nz, _, slots = fr.shape

    def body(cx, carry):
        total = jnp.zeros((PPC * PPC, ny * nz * PPC), jnp.float32)
        for cy in range(ny):
            for cz in range(nz):
                cell = cy * nz + cz
                o = off[cx, cy, cz]
                f = fr[cx, cy, cz]
                kind = sp[cx, cy, cz : cz + 1, :]
                lane = lax.broadcasted_iota(jnp.int32, (1, slots), 1)
                alive = (lane < cnt[(cx * ny + cy) * nz + cz]).astype(jnp.float32)
                charge = table(kind, tchg) * alive
                pos = (o.astype(jnp.float32) + 0.5 + f) / PPC
                zero = jnp.zeros((1, slots), jnp.float32)
                pk_ref[cx, cy, :, cz * slots : (cz + 1) * slots] = jnp.concatenate(
                    [
                        pos,
                        table(kind, tden) * alive,
                        table(kind, tpair) * alive,
                        alive,
                        table(kind, temb),
                        zero,
                    ],
                    axis=0,
                )
                wx, _ = weights_of(o[0:1], f[0:1])
                wy, _ = weights_of(o[1:2], f[1:2])
                wz, _ = weights_of(o[2:3], f[2:3])
                wx = wx * charge
                plane = (wy[:, None, :] * wx[None, :, :]).reshape(PPC * PPC, slots)
                ph, pw = split2(plane)
                zh, zw = split2(placed(wz, cell, ny * nz))
                total = total + mm(
                    jnp.concatenate([ph, pw], axis=1), jnp.concatenate([zh, zh], axis=1), NT
                )
                total = total + mm(ph, zw, NT)
        s_ref[:, pl.ds(pl.multiple_of(cx * PPC, PPC), PPC), :] = total.reshape(
            PPC, PPC, ny * nz * PPC
        )
        return carry

    lax.fori_loop(0, nx, body, 0)


def xmodes_kernel(direct, r_ref, qh, ql, h_ref):
    gx, ys, xs, lanes = r_ref.shape
    q = (qh[...], ql[...])
    for y in range(ys):
        data = r_ref[:, y].reshape(gx * xs, lanes)
        out = mm3(q, split2(data))
        if direct:
            h_ref[:, y] = out.reshape(h_ref.shape[0], h_ref.shape[2], lanes)
        else:
            h_ref[y] = out


def xback_kernel(direct, h_ref, qh, ql, p_ref):
    gx, ys, xs, lanes = p_ref.shape
    q = (qh[...], ql[...])
    for y in range(ys):
        data = h_ref[:, y].reshape(gx * xs, lanes) if direct else h_ref[y]
        out = mm3(q, split2(data))
        p_ref[:, y] = out.reshape(gx, xs, lanes)


def plane_kernel(t_ref, wh, wl, kh, kl, green, o_ref):
    groups, gz, sub, lanes = t_ref.shape
    rows = groups * sub
    lz = green.shape[1]
    ny = wh.shape[1] // lz
    data = jnp.concatenate([t_ref[:, g].reshape(rows, lanes) for g in range(gz)], axis=1)
    u = mm3(split2(data), (wh[...], wl[...]))
    u = jnp.concatenate([u[:, c * lz : (c + 1) * lz] for c in range(ny)], axis=0)
    k = (kh[...], kl[...])
    v = mm3(k, split2(u)) * green[...]
    u = mm3(k, split2(v))
    u = jnp.concatenate([u[c * rows : (c + 1) * rows] for c in range(ny)], axis=1)
    out = mm3(split2(u), (wh[...], wl[...]), NT)
    for g in range(gz):
        o_ref[:, g] = out[:, g * lanes : (g + 1) * lanes].reshape(groups, sub, lanes)


def sample_kernel(cnt, off, fr, sp, tchg, phi_ref, eam, out_ref):
    nx, ny, nz, _, slots = fr.shape

    def body(cx, carry):
        phi = phi_ref[:, pl.ds(pl.multiple_of(cx * PPC, PPC), PPC), :].reshape(
            PPC * PPC, ny * nz * PPC
        )
        ph, pw = split2(phi)
        both = jnp.concatenate([ph, pw], axis=1)
        for cy in range(ny):
            for cz in range(nz):
                cell = cy * nz + cz
                o = off[cx, cy, cz]
                f = fr[cx, cy, cz]
                kind = sp[cx, cy, cz : cz + 1, :]
                lane = lax.broadcasted_iota(jnp.int32, (1, slots), 1)
                alive = (lane < cnt[(cx * ny + cy) * nz + cz]).astype(jnp.float32)
                charge = table(kind, tchg) * alive
                wx, sx = weights_of(o[0:1], f[0:1])
                wy, sy = weights_of(o[1:2], f[1:2])
                wz, sz = weights_of(o[2:3], f[2:3])
                zh, zw = split2(placed(wz, cell, ny * nz))
                sh = placed(sz, cell, ny * nz).astype(jnp.bfloat16)
                right = jnp.concatenate([zh, sh], axis=1)
                g = mm(both, jnp.concatenate([right, right], axis=0))
                gw = g[:, :slots] + mm(ph, zw)
                gs = g[:, slots:]
                fx = jnp.zeros((PPC, slots), jnp.float32)
                fy = jnp.zeros((PPC, slots), jnp.float32)
                fz = jnp.zeros((PPC, slots), jnp.float32)
                for y in range(PPC):
                    a = gw[y * PPC : (y + 1) * PPC]
                    b = gs[y * PPC : (y + 1) * PPC]
                    fx = fx + wy[y : y + 1] * a
                    fy = fy + sy[y : y + 1] * a
                    fz = fz + wy[y : y + 1] * b
                field = jnp.concatenate(
                    [
                        jnp.sum(sx * fx, axis=0, keepdims=True),
                        jnp.sum(wx * fy, axis=0, keepdims=True),
                        jnp.sum(wx * fz, axis=0, keepdims=True),
                    ],
                    axis=0,
                )
                out_ref[cx, cy, cz] = (eam[cx, cy, cz] - COUPLING * charge * field) * alive
        return carry

    lax.fori_loop(0, nx, body, 0)


def centred(ext, ex, ey, first_z, lanes, dims):
    nx, ny, nz = dims
    slots_iota = lax.broadcasted_iota(jnp.int32, (3, lanes), 1)
    row = lax.broadcasted_iota(jnp.int32, (3, lanes), 0)
    cell_z = (slots_iota // 128).astype(jnp.float32) + (
        jnp.asarray(first_z, jnp.int32).astype(jnp.float32) - (1.0 + nz / 2)
    )
    cell_x = jnp.asarray(ex, jnp.int32).astype(jnp.float32) - (1.0 + nx / 2)
    cell_y = jnp.asarray(ey, jnp.int32).astype(jnp.float32) - (1.0 + ny / 2)
    shift = jnp.where(row == 0, cell_x, jnp.where(row == 1, cell_y, cell_z))
    return ext + shift


def density_kernel(ext, den_ref, slope_ref, f_ref, acc):
    ex_n, ey_n, _, lanes = ext.shape
    nx, ny = ex_n - 2, ey_n - 2
    slots = 128
    nz = lanes // slots - 2
    dims = (nx, ny, nz)

    def build(index, carry):
        ex, ey = index // ey_n, index % ey_n
        q = centred(ext[ex, ey, 0:3, :], ex, ey, 0, lanes, dims)
        h, m, l = split3(q)
        n = jnp.sum(q * q, axis=0, keepdims=True)
        nh, nm, nl = split3(-n)
        one = jnp.ones((3, lanes), jnp.float32)
        zero = jnp.zeros((KF - 24, lanes), jnp.float32)
        f_ref[index] = jnp.concatenate(
            [2 * h, 2 * m, 2 * h, 2 * l, 2 * h, 2 * m, nh, nm, nl, one, zero], axis=0
        ).astype(jnp.bfloat16)
        return carry

    lax.fori_loop(0, ex_n * ey_n, build, 0)

    def cell(index, carry):
        ix = index // (ny * nz)
        iy = (index // nz) % ny
        iz = index % nz
        start = pl.multiple_of(iz * slots, slots)
        own = ext[ix + 1, iy + 1, :, pl.ds(start + slots, slots)]
        left = own_features(own, ix, iy, iz, dims)
        acc[...] = jnp.zeros_like(acc)
        for dx in range(3):
            for dy in range(3):
                wide = pl.ds(start, 3 * slots)
                d = mm(left, f_ref[(ix + dx) * ey_n + iy + dy, :, wide])
                coef = ext[ix + dx, iy + dy, 3:4, wide]
                w = jnp.maximum(d, 0.0)
                term = w * w * w * coef
                acc[...] += term[:, :slots] + term[:, slots : 2 * slots] + term[:, 2 * slots :]
        total = jnp.sum(acc[...].T, axis=0, keepdims=True)
        alive = own[5:6]
        density = (total - own[3:4]) * alive
        den_ref[ix, iy, pl.ds(iz, 1), :] = density
        slope_ref[ix, iy, :, pl.ds(start, slots)] = (
            -own[6:7] * alive / (2.0 * jnp.sqrt(1.0 + density))
        )
        return carry

    lax.fori_loop(0, nx * ny * nz, cell, 0)


def own_features(own, ix, iy, iz, dims):
    slots = own.shape[1]
    q = centred(own[0:3], ix + 1, iy + 1, iz + 1, slots, dims)
    h, m, l = split3(q)
    nh, nm, nl = split3(1.0 - jnp.sum(q * q, axis=0, keepdims=True))
    one = jnp.ones((3, slots), jnp.float32)
    zero = jnp.zeros((slots - 24, slots), jnp.float32)
    rows = jnp.concatenate([h, h, m, h, l, m, one, nh, nm, nl, zero], axis=0)
    return rows.T[:, :KF].astype(jnp.bfloat16)


def force_kernel(ext, slope, f_ref, out_ref, rows_ref, acc, mine):
    ex_n, ey_n, _, lanes = ext.shape
    nx, ny = ex_n - 2, ey_n - 2
    slots = 128
    nz = lanes // slots - 2
    dims = (nx, ny, nz)

    def build(index, carry):
        ex, ey = index // ey_n, index % ey_n
        block = ext[ex, ey]
        q = centred(block[0:3], ex, ey, 0, lanes, dims)
        c = block[3:4]
        inv = jnp.where(c > 0.0, 1.0 / jnp.where(c > 0.0, c, 1.0), 0.0)
        rho = block[4:5] * inv
        t = -6.0 * slope[ex, ey] * inv
        rows_ref[index] = jnp.concatenate([c * q, c, rho, t, jnp.zeros((2, lanes), jnp.float32)], 0)
        return carry

    lax.fori_loop(0, ex_n * ey_n, build, 0)

    def cell(index, carry):
        ix = index // (ny * nz)
        iy = (index // nz) % ny
        iz = index % nz
        start = pl.multiple_of(iz * slots, slots)
        own = ext[ix + 1, iy + 1, :, pl.ds(start + slots, slots)]
        left = own_features(own, ix, iy, iz, dims)
        own_rows = rows_ref[(ix + 1) * ey_n + iy + 1, :, pl.ds(start + slots, slots)]
        rho = jnp.broadcast_to(-4.0 * own_rows[4:5], (slots, slots))
        mine[0] = rho.T
        mine[1] = jnp.broadcast_to(own_rows[5:6], (slots, slots)).T
        acc[...] = jnp.zeros_like(acc)
        for dx in range(3):
            for dy in range(3):
                row = (ix + dx) * ey_n + iy + dy
                wide = pl.ds(start, 3 * slots)
                d = mm(left, f_ref[row, :, wide])
                near = rows_ref[row, :, wide]
                for part in range(4):
                    size = slots // 4
                    at = slice(part * size, (part + 1) * size)
                    r_i = mine[0, at]
                    t_i = mine[1, at]
                    sums = [jnp.zeros((size, slots), jnp.float32) for _ in range(4)]
                    for k in range(3):
                        lane = slice(k * slots, (k + 1) * slots)
                        w = jnp.maximum(d[at, lane], 0.0)
                        value = w * (r_i * near[4:5, lane] + w * (t_i + near[5:6, lane]))
                        for a in range(4):
                            sums[a] = sums[a] + value * near[a : a + 1, lane]
                    for a in range(4):
                        acc[a, at] += sums[a]
        total = [jnp.sum(acc[a].T, axis=0, keepdims=True) for a in range(4)]
        q = centred(own[0:3], ix + 1, iy + 1, iz + 1, slots, dims)
        out_ref[ix, iy, iz] = own[3:4] * (jnp.concatenate(total[:3], axis=0) - q * total[3])
        return carry

    lax.fori_loop(0, nx * ny * nz, cell, 0)


def hartley(length):
    index = np.arange(length)
    phase = (np.outer(index, index) % length) * (2.0 * np.pi / length)
    return (np.cos(phase) + np.sin(phase)) / np.sqrt(length)


def halves(values):
    high = values.astype(np.float32).astype(jnp.bfloat16)
    low = (values - high.astype(np.float64)).astype(np.float32).astype(jnp.bfloat16)
    return jnp.asarray(high), jnp.asarray(low)


def call(kernel, out_shape, args, scalars=(), scratch=(), flops=1000000):
    specs = [SM if i in scalars else VM for i in range(len(args))]
    outs = jax.tree.map(lambda _: VM, out_shape)
    return pl.pallas_call(
        kernel,
        out_shape=out_shape,
        in_specs=specs,
        out_specs=outs,
        scratch_shapes=list(scratch),
        compiler_params=pltpu.CompilerParams(vmem_limit_bytes=48 * 1024 * 1024),
        cost_estimate=pl.CostEstimate(flops=flops, bytes_accessed=2000000, transcendentals=0),
    )(*args)


def on_device(cell_counts, grid_offset, fraction, species, t_den, t_pair, t_emb, t_chg):
    f32 = jnp.float32
    nx, ny, nz, _, slots = fraction.shape
    gx, gy, gz = (lax.axis_size(a) for a in ("gx", "gy", "gz"))
    every = ("gx", "gy", "gz")
    n_dev = gx * gy * gz
    lx, ly, lz = gx * nx * PPC, gy * ny * PPC, gz * nz * PPC
    xs = nx * PPC
    lanes = ny * nz * PPC
    ys = PPC // gx
    modes = lx // n_dev
    counts = cell_counts.reshape(-1)

    sds = jax.ShapeDtypeStruct
    charge, packed = call(
        spread_kernel,
        (sds((PPC, xs, lanes), f32), sds((nx, ny, 8, nz * slots), f32)),
        (counts, grid_offset, fraction, species, t_den, t_pair, t_emb, t_chg),
        scalars=(0, 4, 5, 6, 7),
    )
    sides = (("gz", 3), ("gy", 1), ("gx", 0))
    ext = padded(packed, sides, (slots, 1, 1))

    qh, ql = halves(hartley(lx))
    zmat = hartley(lz)
    cut = nz * PPC
    wide = np.zeros((gz, ny, cut, ny, lz))
    for c in range(ny):
        wide[:, c, :, c, :] = zmat.reshape(gz, cut, lz)
    wh, wl = halves(wide.reshape(gz * lanes, ny * lz))
    order = (
        np.arange(ly).reshape(gy, ny, gx, ys).transpose(1, 2, 0, 3).reshape(-1)
    )
    kron = np.kron(hartley(ly)[np.ix_(order, order)], np.eye(modes))
    kh, kl = halves(kron)

    def wave(index, length):
        return np.minimum(index, length - index) * (2.0 * math.pi / length)

    wave_y = np.repeat(wave(order, ly), modes).astype(np.float32)[:, None]
    wave_z = wave(np.arange(lz), lz).astype(np.float32)[None, :]
    mode_x = lax.axis_index(every) * modes + jnp.asarray(
        np.tile(np.arange(modes, dtype=np.int32), ly)[:, None]
    )
    wave_x = jnp.minimum(mode_x, lx - mode_x).astype(f32) * (2.0 * math.pi / lx)
    square = wave_x * wave_x + wave_y * wave_y + wave_z * wave_z
    anchor = square == 0.0
    green = jnp.where(
        anchor,
        0.0,
        4.0
        * math.pi
        * jnp.exp(-square / (4.0 * EWALD_SPLIT * EWALD_SPLIT))
        / jnp.where(anchor, 1.0, square),
    )

    direct = modes % 8 == 0
    got = lax.all_to_all(charge.reshape(gx, ys * xs, lanes), "gx", 0, 0, tiled=True)
    got = got.reshape(gx, ys, xs, lanes)
    import functools

    mid = sds((n_dev, ys, modes, lanes) if direct else (ys, lx, lanes), f32)
    modal = call(functools.partial(xmodes_kernel, direct), mid, (got, qh, ql))
    if not direct:
        modal = modal.reshape(ys, n_dev, modes, lanes).transpose(1, 0, 2, 3)
    modal = lax.all_to_all(modal.reshape(n_dev, ys * modes, lanes), every, 0, 0, tiled=True)

    density, slope, feats = call(
        density_kernel,
        (
            sds((nx, ny, nz, slots), f32),
            sds((nx, ny, 1, nz * slots), f32),
            sds(((nx + 2) * (ny + 2), KF, (nz + 2) * slots), jnp.bfloat16),
        ),
        (ext,),
        scratch=(pltpu.VMEM((slots, slots), f32),),
        flops=400000000,
    )
    ext_slope = padded(slope, sides, (slots, 1, 1))

    planes = call(
        plane_kernel,
        sds((gx * gy, gz, ys * modes, lanes), f32),
        (modal.reshape(gx * gy, gz, ys * modes, lanes), wh, wl, kh, kl, green),
    )
    back = lax.all_to_all(planes.reshape(n_dev, ys * modes, lanes), every, 0, 0, tiled=True)
    back = back.reshape(n_dev, ys, modes, lanes)
    if not direct:
        back = back.transpose(1, 0, 2, 3).reshape(ys, lx, lanes)
    lines = call(
        functools.partial(xback_kernel, direct), sds((gx, ys, xs, lanes), f32), (back, qh, ql)
    )
    eam = call(
        force_kernel,
        sds((nx, ny, nz, 3, slots), f32),
        (ext, ext_slope, feats),
        scratch=(
            pltpu.VMEM(((nx + 2) * (ny + 2), 8, (nz + 2) * slots), f32),
            pltpu.VMEM((4, slots, slots), f32),
            pltpu.VMEM((2, slots, slots), f32),
        ),
        flops=800000000,
    )
    phi = lax.all_to_all(lines.reshape(gx, ys * xs, lanes), "gx", 0, 0, tiled=True)
    forces = call(
        sample_kernel,
        sds((nx, ny, nz, 3, slots), f32),
        (counts, grid_offset, fraction, species, t_chg, phi.reshape(PPC, xs, lanes), eam),
        scalars=(0, 4),
    )
    return (forces, density)


def solution(mesh):
    return jax.shard_map(
        on_device,
        mesh=mesh,
        in_specs=(
            P("gx", "gy", "gz"),
            P("gx", "gy", "gz", None, None),
            P("gx", "gy", "gz", None, None),
            P("gx", "gy", "gz", None),
            P(),
            P(),
            P(),
            P(),
        ),
        out_specs=(P("gx", "gy", "gz", None, None), P("gx", "gy", "gz", None)),
        check_vma=False,
    )
```

time: 477 us -> 164 us (0.34)
  the two profiles are of different devices: /device:TPU:1 before, /device:TPU:0 now
where the time goes in v1:
time: 164 us; the launch traced here: 163 us
  Pallas kernels  72.2 us (44%)
  waiting for transfers between devices  28.7 us (18%)
  starting transfers between devices  25.7 us (16%)
  blocking collectives  20.6 us (13%)
  local copies, waits for them, and re-layouts  12.4 us (8%)
  other arithmetic  2.14 us (1%)
    pallas_call x7, Pallas kernels, call(): pl.pallas_call(kernel, out_shape=out_shape, in_specs=specs, out_specs=out...  72.2 us
    all_to_all x1, blocking collectives, on_device(): lax.all_to_all(charge.reshape(gx, ys * xs, lanes), 'gx', 0, 0, tiled=True)  20.6 us
    ppermute x6, waiting for transfers between devices, padded(): lax.ppermute(lax.slice_in_dim(block, block.shape[dim] - width, None, axis...  18.6 us
    unnamed x41, local copies, waits for them, and re-layouts  8.64 us
    ppermute x6, starting transfers between devices, padded(): lax.ppermute(lax.slice_in_dim(block, 0, width, axis=dim), axis, backward)  8.3 us
    ppermute x6, starting transfers between devices, padded(): lax.ppermute(lax.slice_in_dim(block, block.shape[dim] - width, None, axis...  6.93 us
    all_to_all x1, waiting for transfers between devices, on_device(): lax.all_to_all(modal.reshape(n_dev, ys * modes, lanes), every, 0, 0, tile...  6.01 us
    ppermute x6, waiting for transfers between devices, padded(): lax.ppermute(lax.slice_in_dim(block, 0, width, axis=dim), axis, backward)  4.14 us
  transfers between devices with their start and end apart: 15, of which 9 were waited for; matrix products, arithmetic and copies ran while one was open for 5% of the time, Pallas kernels for 40%

profile of v1, /device:TPU:0, one launch (start us, length us, event | category | flops | bytes accessed | tf_op | source)
XLA Modules:
  0.0 162.9 jit_solution(1871283845707381849)
XLA Ops:
  6.5 2.9 %shard_map.176 = (f32[16,64,128]{2,1,0:T(8,128)S(1)}, f32[4,2,8,512]{3,2,1,0:T(8,128)S(1)}) custom-call(s32[32]{0:T(128)S(1)} %reshape.31.cnt, s32[4,2,4,3,128]{4,3,2,1,0:T(4,128)S(1)} %copy.26.off, f32[4,2,4,3,128]{4,3,2,1,0:T(4,128)S(1)} %copy.27.fr, s32[4,2,4,128]{3,2,1,0:T(4,128)S(1)} %copy-done.7, f32[2]{0:T(128)S(1)} %copy-done.11, f32[2]{0:T(128)S(1)} %copy-done.12, ...), custom_call_target="tpu_custom_call" | custom-call | flops 1000000 | bytes 2000000 | tf_op jit(solution)/shard_map/pallas_call | solution.py:366
  9.4 20.6 %all_to_all.20 = f32[4,256,128]{2,1,0:T(8,128)S(1)} all-to-all(f32[4,256,128]{2,1,0:T(8,128)S(1)} %bitcast.13), channel_id=1, replica_groups=mesh['gx'=4,'gy'=2,'gz'=4] {'gx'}, dimensions={0} | all-to-all | bytes 1048576 | tf_op jit(solution)/shard_map/all_to_all | solution.py:434
  30.1 1.3 shard_map.177
  31.4 3.7 %all-to-all-start.1 = ((f32[32,32,128]{2,1,0:T(8,128)}), f32[32,32,128]{2,1,0:T(8,128)S(1)}, u32[]{:S(2)}, u32[]{:S(2)}) async-start(f32[32,32,128]{2,1,0:T(8,128)} %bitcast.2), calls=%async_computation.1 | async-start | bytes 1048576 | tf_op jit(solution)/shard_map/all_to_all | solution.py:442
  35.8 1.5 collective-permute-start.1
  37.6 4.2 %collective-permute-done = f32[4,2,8,128]{3,2,1,0:T(8,128)} collective-permute-done((f32[4,2,8,128]{3,2,1,0:T(8,128)}, f32[4,2,8,128]{3,2,1,0:T(8,128)}, u32[]{:S(2)}, u32[]{:S(2)}) %collective-permute-start) | collective-permute-done | bytes 32800 | tf_op jit(solution)/shard_map/ppermute | solution.py:26
  41.8 1.4 constant_dynamic-update-slice_fusion.2
  43.1 1.6 constant_dynamic-update-slice_fusion.1
  44.7 6.0 %all-to-all-done.1 = f32[32,32,128]{2,1,0:T(8,128)S(1)} async-done(((f32[32,32,128]{2,1,0:T(8,128)}), f32[32,32,128]{2,1,0:T(8,128)S(1)}, u32[]{:S(2)}, u32[]{:S(2)}) %all-to-all-start.1) | async-done | bytes 524320 | tf_op jit(solution)/shard_map/all_to_all | solution.py:442
  50.8 3.6 %shard_map.178 = f32[8,4,32,128]{3,2,1,0:T(8,128)} custom-call(f32[8,4,32,128]{3,2,1,0:T(8,128)S(1)} %bitcast.9, bf16[512,512]{1,0:T(8,128)(2,1)S(1)} %copy-done.3, bf16[512,512]{1,0:T(8,128)(2,1)S(1)} %copy-done.2, bf16[512,512]{1,0:T(8,128)(2,1)S(1)} %copy-done.1, bf16[512,512]{1,0:T(8,128)(2,1)S(1)} %copy-done, f32[512,256]{1,0:T(8,128)S(1)} %fusion.green), custom_call_target="tpu_custom_call" | custom-call | flops 1000000 | bytes 2000000 | tf_op jit(solution)/shard_map/pallas_call | solution.py:366
  54.3 3.0 %all-to-all-start.2 = ((f32[32,32,128]{2,1,0:T(8,128)}), f32[32,32,128]{2,1,0:T(8,128)S(1)}, u32[]{:S(2)}, u32[]{:S(2)}) async-start(f32[32,32,128]{2,1,0:T(8,128)} %bitcast.5), calls=%async_computation.2 | async-start | bytes 1048576 | tf_op jit(solution)/shard_map/all_to_all | solution.py:462
  57.3 1.4 constant_dynamic-update-slice_fusion
  58.7 1.0 fusion.9
  59.7 1.8 %collective-permute-start.2 = (f32[4,1,8,768]{3,2,1,0:T(8,128)S(1)}, f32[4,1,8,768]{3,2,1,0:T(8,128)S(1)}, u32[]{:S(2)}, u32[]{:S(2)}) collective-permute-start(f32[4,1,8,768]{3,2,1,0:T(8,128)S(1)} %get-tuple-element.18), channel_id=1, source_target_pairs={{0,4},{4,0},{1,5},{5,1},{2,6},{6,2},{3,7},{7,3},{8,12},{12,8},{9,1... | collective-permute-start | bytes 294920 | tf_op jit(solution)/shard_map/ppermute | solution.py:26
  61.7 5.5 %collective-permute-done.2 = f32[4,1,8,768]{3,2,1,0:T(8,128)S(1)} collective-permute-done((f32[4,1,8,768]{3,2,1,0:T(8,128)S(1)}, f32[4,1,8,768]{3,2,1,0:T(8,128)S(1)}, u32[]{:S(2)}, u32[]{:S(2)}) %collective-permute-start.2) | collective-permute-done | bytes 98336 | tf_op jit(solution)/shard_map/ppermute | solution.py:26
  67.2 2.3 %collective-permute-done.3 = f32[4,1,8,768]{3,2,1,0:T(8,128)S(1)} collective-permute-done((f32[4,1,8,768]{3,2,1,0:T(8,128)S(1)}, f32[4,1,8,768]{3,2,1,0:T(8,128)S(1)}, u32[]{:S(2)}, u32[]{:S(2)}) %collective-permute-start.3) | collective-permute-done | bytes 98336 | tf_op jit(solution)/shard_map/ppermute | solution.py:29
  70.3 2.1 %collective-permute-start.4 = (f32[1,4,8,768]{3,2,1,0:T(8,128)S(1)}, f32[1,4,8,768]{3,2,1,0:T(8,128)S(1)}, u32[]{:S(2)}, u32[]{:S(2)}) collective-permute-start(f32[1,4,8,768]{3,2,1,0:T(8,128)S(1)} %get-tuple-element.16), channel_id=1, source_target_pairs={{0,8},{8,16},{16,24},{24,0},{1,9},{9,17},{17,25},{25,1},{2,10},{10... | collective-permute-start | bytes 294920 | tf_op jit(solution)/shard_map/ppermute | solution.py:26
  72.4 1.8 %collective-permute-start.5 = (f32[1,4,8,768]{3,2,1,0:T(8,128)S(1)}, f32[1,4,8,768]{3,2,1,0:T(8,128)S(1)}, u32[]{:S(2)}, u32[]{:S(2)}) collective-permute-start(f32[1,4,8,768]{3,2,1,0:T(8,128)S(1)} %get-tuple-element.17), channel_id=1, source_target_pairs={{8,0},{16,8},{24,16},{0,24},{9,1},{17,9},{25,17},{1,25},{10,2},{18... | collective-permute-start | bytes 294920 | tf_op jit(solution)/shard_map/ppermute | solution.py:29
  74.2 3.3 %collective-permute-done.4 = f32[1,4,8,768]{3,2,1,0:T(8,128)S(1)} collective-permute-done((f32[1,4,8,768]{3,2,1,0:T(8,128)S(1)}, f32[1,4,8,768]{3,2,1,0:T(8,128)S(1)}, u32[]{:S(2)}, u32[]{:S(2)}) %collective-permute-start.4) | collective-permute-done | bytes 98336 | tf_op jit(solution)/shard_map/ppermute | solution.py:26
  77.4 1.0 collective-permute-done.5
  78.5 1.0 pad_maximum_fusion.ext
  79.4 21.9 %shard_map.180 = (f32[4,2,4,128]{3,2,1,0:T(4,128)}, f32[4,2,1,512]{3,2,1,0:T(1,128)S(1)}, bf16[24,32,768]{2,1,0:T(8,128)(2,1)S(1)}) custom-call(f32[6,4,8,768]{3,2,1,0:T(8,128)S(1)} %pad_maximum_fusion.ext), custom_call_target="tpu_custom_call" | custom-call | flops 400000000 | bytes 2000000 | tf_op jit(solution)/shard_map/pallas_call | solution.py:366
  101.3 1.7 %collective-permute-start.7 = (f32[4,2,1,128]{3,2,1,0:T(1,128)S(1)}, f32[4,2,1,128]{3,2,1,0:T(1,128)S(1)}, u32[]{:S(2)}, u32[]{:S(2)}) collective-permute-start(f32[4,2,1,128]{3,2,1,0:T(1,128)S(1)} %get-tuple-element.26), channel_id=1, source_target_pairs={{1,0},{2,1},{3,2},{0,3},{5,4},{6,5},{7,6},{4,7},{9,8},{10,9},{11,1... | collective-permute-start | bytes 12296 | tf_op jit(solution)/shard_map/ppermute | solution.py:29
  103.1 1.3 shard_map.179
  104.4 3.8 %all-to-all-start.3 = ((f32[4,256,128]{2,1,0:T(8,128)}), f32[4,256,128]{2,1,0:T(8,128)S(1)}, u32[]{:S(2)}, u32[]{:S(2)}) async-start(f32[4,256,128]{2,1,0:T(8,128)} %bitcast.7), calls=%async_computation.3 | async-start | bytes 1048576 | tf_op jit(solution)/shard_map/all_to_all | solution.py:480
  109.2 1.2 collective-permute-start.9
  110.4 1.7 %collective-permute-done.8 = f32[4,1,1,768]{3,2,1,0:T(1,128)S(1)} collective-permute-done((f32[4,1,1,768]{3,2,1,0:T(1,128)S(1)}, f32[4,1,1,768]{3,2,1,0:T(1,128)S(1)}, u32[]{:S(2)}, u32[]{:S(2)}) %collective-permute-start.8) | collective-permute-done | bytes 12320 | tf_op jit(solution)/shard_map/ppermute | solution.py:26
  112.9 2.1 %collective-permute-start.10 = (f32[1,4,1,768]{3,2,1,0:T(1,128)S(1)}, f32[1,4,1,768]{3,2,1,0:T(1,128)S(1)}, u32[]{:S(2)}, u32[]{:S(2)}) collective-permute-start(f32[1,4,1,768]{3,2,1,0:T(1,128)S(1)} %get-tuple-element.22), channel_id=1, source_target_pairs={{0,8},{8,16},{16,24},{24,0},{1,9},{9,17},{17,25},{25,1},{2,10},{10... | collective-permute-start | bytes 36872 | tf_op jit(solution)/shard_map/ppermute | solution.py:26
  115.0 1.9 %collective-permute-start.11 = (f32[1,4,1,768]{3,2,1,0:T(1,128)S(1)}, f32[1,4,1,768]{3,2,1,0:T(1,128)S(1)}, u32[]{:S(2)}, u32[]{:S(2)}) collective-permute-start(f32[1,4,1,768]{3,2,1,0:T(1,128)S(1)} %get-tuple-element.23), channel_id=1, source_target_pairs={{8,0},{16,8},{24,16},{0,24},{9,1},{17,9},{25,17},{1,25},{10,2},{18... | collective-permute-start | bytes 36872 | tf_op jit(solution)/shard_map/ppermute | solution.py:29
  116.9 4.0 %collective-permute-done.10 = f32[1,4,1,768]{3,2,1,0:T(1,128)S(1)} collective-permute-done((f32[1,4,1,768]{3,2,1,0:T(1,128)S(1)}, f32[1,4,1,768]{3,2,1,0:T(1,128)S(1)}, u32[]{:S(2)}, u32[]{:S(2)}) %collective-permute-start.10) | collective-permute-done | bytes 12320 | tf_op jit(solution)/shard_map/ppermute | solution.py:26
  120.9 38.3 %shard_map.181.eam = f32[4,2,4,3,128]{4,3,2,1,0:T(4,128)S(1)} custom-call(f32[6,4,8,768]{3,2,1,0:T(8,128)S(1)} %pad_maximum_fusion.ext, f32[6,4,1,768]{3,2,1,0:T(1,128)S(1)} %pad_maximum_fusion.4.slope, bf16[24,32,768]{2,1,0:T(8,128)(2,1)S(1)} %get-tuple-element.10.f_ref), custom_call_target="tpu_custom_call" | custom-call | flops 800000000 | bytes 2000000 | tf_op jit(solution)/shard_map/pallas_call | solution.py:366
  159.3 2.9 %shard_map.182 = f32[4,2,4,3,128]{4,3,2,1,0:T(4,128)S(1)} custom-call(s32[32]{0:T(128)S(1)} %reshape.31.cnt, s32[4,2,4,3,128]{4,3,2,1,0:T(4,128)S(1)} %copy.26.off, f32[4,2,4,3,128]{4,3,2,1,0:T(4,128)S(1)} %copy.27.fr, s32[4,2,4,128]{3,2,1,0:T(4,128)S(1)} %copy-done.8, f32[2]{0:T(128)S(1)} %copy-done.10, f32[16,64,128]{2,1,0:T(8,128)S(1)} %bitcast.10, ...), custom_call_target="tpu_custom_call" | custom-call | flops 1000000 | bytes 2000000 | tf_op jit(solution)/shard_map/pallas_call | solution.py:366
  (60 shorter events, 10.4 us)
Async XLA Ops:
  0.6 29.4 %copy-start.4 = (bf16[256,256]{1,0:T(8,128)(2,1)S(1)}, bf16[256,256]{1,0:T(8,128)(2,1)}, u32[]{:S(2)}) copy-start(bf16[256,256]{1,0:T(8,128)(2,1)} %constant.49.clone.ql) | copy-start | bytes 393220
  0.6 29.4 %copy-start.5 = (bf16[256,256]{1,0:T(8,128)(2,1)S(1)}, bf16[256,256]{1,0:T(8,128)(2,1)}, u32[]{:S(2)}) copy-start(bf16[256,256]{1,0:T(8,128)(2,1)} %constant.48.clone.qh) | copy-start | bytes 393220
  3.1 0.7 copy-start.7
  3.8 0.7 copy-start.9
  4.5 0.7 copy-start.11
  5.1 0.7 copy-start.12
  5.8 0.7 copy-start.13
  9.4 25.8 %copy-start.6 = (f32[4,2,8,512]{3,2,1,0:T(8,128)}, f32[4,2,8,512]{3,2,1,0:T(8,128)S(1)}, u32[]{:S(2)}) copy-start(f32[4,2,8,512]{3,2,1,0:T(8,128)S(1)} %get-tuple-element.8) | copy-start | bytes 393220
  30.0 7.2 %copy-start.14 = (f32[512,1]{0,1:T(1,128)S(1)}, f32[512,1]{0,1:T(1,128)}, u32[]{:S(2)}) copy-start(f32[512,1]{0,1:T(1,128)} %constant.55.clone) | copy-start | bytes 6148
  30.0 7.2 %copy-start.15 = (s32[512,1]{0,1:T(1,128)S(1)}, s32[512,1]{0,1:T(1,128)}, u32[]{:S(2)}) copy-start(s32[512,1]{0,1:T(1,128)} %constant.54.clone) | copy-start | bytes 6148
  30.0 7.3 %copy-start.16 = (f32[256]{0:T(256)S(1)}, f32[256]{0:T(256)}, u32[]{:S(2)}) copy-start(f32[256]{0:T(256)} %constant.57) | copy-start | bytes 3076
  30.0 20.7 %copy-start.3 = (bf16[512,512]{1,0:T(8,128)(2,1)S(1)}, bf16[512,512]{1,0:T(8,128)(2,1)}, u32[]{:S(2)}) copy-start(bf16[512,512]{1,0:T(8,128)(2,1)} %constant.50.clone.wh) | copy-start | bytes 1572868
  31.4 19.3 %copy-start = (bf16[512,512]{1,0:T(8,128)(2,1)S(1)}, bf16[512,512]{1,0:T(8,128)(2,1)}, u32[]{:S(2)}) copy-start(bf16[512,512]{1,0:T(8,128)(2,1)} %constant.53.clone.kl) | copy-start | bytes 1572868
  31.4 19.3 %copy-start.1 = (bf16[512,512]{1,0:T(8,128)(2,1)S(1)}, bf16[512,512]{1,0:T(8,128)(2,1)}, u32[]{:S(2)}) copy-start(bf16[512,512]{1,0:T(8,128)(2,1)} %constant.52.clone.kh) | copy-start | bytes 1572868
  31.4 19.3 %copy-start.2 = (bf16[512,512]{1,0:T(8,128)(2,1)S(1)}, bf16[512,512]{1,0:T(8,128)(2,1)}, u32[]{:S(2)}) copy-start(bf16[512,512]{1,0:T(8,128)(2,1)} %constant.51.clone.wl) | copy-start | bytes 1572868
  31.4 19.3 %all-to-all-start.1 = ((f32[32,32,128]{2,1,0:T(8,128)}), f32[32,32,128]{2,1,0:T(8,128)S(1)}, u32[]{:S(2)}, u32[]{:S(2)}) async-start(f32[32,32,128]{2,1,0:T(8,128)} %bitcast.2), calls=%async_computation.1 | async-start | bytes 1048576 | tf_op jit(solution)/shard_map/all_to_all | solution.py:442
  35.8 21.5 %collective-permute-start.1 = (f32[4,2,8,128]{3,2,1,0:T(8,128)}, f32[4,2,8,128]{3,2,1,0:T(8,128)}, u32[]{:S(2)}, u32[]{:S(2)}) collective-permute-start(f32[4,2,8,128]{3,2,1,0:T(8,128)} %get-tuple-element.20), channel_id=1, source_target_pairs={{1,0},{2,1},{3,2},{0,3},{5,4},{6,5},{7,6},{4,7},{9,8},{10,9},{11,1... | collective-permute-start | bytes 98312 | tf_op jit(solution)/shard_map/ppermute | solution.py:29
  37.3 4.5 %collective-permute-start = (f32[4,2,8,128]{3,2,1,0:T(8,128)}, f32[4,2,8,128]{3,2,1,0:T(8,128)}, u32[]{:S(2)}, u32[]{:S(2)}) collective-permute-start(f32[4,2,8,128]{3,2,1,0:T(8,128)} %get-tuple-element.21), channel_id=1, source_target_pairs={{0,1},{1,2},{2,3},{3,0},{4,5},{5,6},{6,7},{7,4},{8,9},{9,10},{10,1... | collective-permute-start | bytes 98312 | tf_op jit(solution)/shard_map/ppermute | solution.py:26
  54.3 48.7 %all-to-all-start.2 = ((f32[32,32,128]{2,1,0:T(8,128)}), f32[32,32,128]{2,1,0:T(8,128)S(1)}, u32[]{:S(2)}, u32[]{:S(2)}) async-start(f32[32,32,128]{2,1,0:T(8,128)} %bitcast.5), calls=%async_computation.2 | async-start | bytes 1048576 | tf_op jit(solution)/shard_map/all_to_all | solution.py:462
  59.7 7.5 %collective-permute-start.2 = (f32[4,1,8,768]{3,2,1,0:T(8,128)S(1)}, f32[4,1,8,768]{3,2,1,0:T(8,128)S(1)}, u32[]{:S(2)}, u32[]{:S(2)}) collective-permute-start(f32[4,1,8,768]{3,2,1,0:T(8,128)S(1)} %get-tuple-element.18), channel_id=1, source_target_pairs={{0,4},{4,0},{1,5},{5,1},{2,6},{6,2},{3,7},{7,3},{8,12},{12,8},{9,1... | collective-permute-start | bytes 294920 | tf_op jit(solution)/shard_map/ppermute | solution.py:26
  61.5 8.0 %collective-permute-start.3 = (f32[4,1,8,768]{3,2,1,0:T(8,128)S(1)}, f32[4,1,8,768]{3,2,1,0:T(8,128)S(1)}, u32[]{:S(2)}, u32[]{:S(2)}) collective-permute-start(f32[4,1,8,768]{3,2,1,0:T(8,128)S(1)} %get-tuple-element.19), channel_id=1, source_target_pairs={{4,0},{0,4},{5,1},{1,5},{6,2},{2,6},{7,3},{3,7},{12,8},{8,12},{13,... | collective-permute-start | bytes 294920 | tf_op jit(solution)/shard_map/ppermute | solution.py:29
  70.3 7.1 %collective-permute-start.4 = (f32[1,4,8,768]{3,2,1,0:T(8,128)S(1)}, f32[1,4,8,768]{3,2,1,0:T(8,128)S(1)}, u32[]{:S(2)}, u32[]{:S(2)}) collective-permute-start(f32[1,4,8,768]{3,2,1,0:T(8,128)S(1)} %get-tuple-element.16), channel_id=1, source_target_pairs={{0,8},{8,16},{16,24},{24,0},{1,9},{9,17},{17,25},{25,1},{2,10},{10... | collective-permute-start | bytes 294920 | tf_op jit(solution)/shard_map/ppermute | solution.py:26
  72.4 6.1 %collective-permute-start.5 = (f32[1,4,8,768]{3,2,1,0:T(8,128)S(1)}, f32[1,4,8,768]{3,2,1,0:T(8,128)S(1)}, u32[]{:S(2)}, u32[]{:S(2)}) collective-permute-start(f32[1,4,8,768]{3,2,1,0:T(8,128)S(1)} %get-tuple-element.17), channel_id=1, source_target_pairs={{8,0},{16,8},{24,16},{0,24},{9,1},{17,9},{25,17},{1,25},{10,2},{18... | collective-permute-start | bytes 294920 | tf_op jit(solution)/shard_map/ppermute | solution.py:29
  101.3 6.9 %collective-permute-start.6 = (f32[4,2,1,128]{3,2,1,0:T(1,128)S(1)}, f32[4,2,1,128]{3,2,1,0:T(1,128)S(1)}, u32[]{:S(2)}, u32[]{:S(2)}) collective-permute-start(f32[4,2,1,128]{3,2,1,0:T(1,128)S(1)} %get-tuple-element.27), channel_id=1, source_target_pairs={{0,1},{1,2},{2,3},{3,0},{4,5},{5,6},{6,7},{7,4},{8,9},{9,10},{10,1... | collective-permute-start | bytes 12296 | tf_op jit(solution)/shard_map/ppermute | solution.py:26
  101.3 6.9 %collective-permute-start.7 = (f32[4,2,1,128]{3,2,1,0:T(1,128)S(1)}, f32[4,2,1,128]{3,2,1,0:T(1,128)S(1)}, u32[]{:S(2)}, u32[]{:S(2)}) collective-permute-start(f32[4,2,1,128]{3,2,1,0:T(1,128)S(1)} %get-tuple-element.26), channel_id=1, source_target_pairs={{1,0},{2,1},{3,2},{0,3},{5,4},{6,5},{7,6},{4,7},{9,8},{10,9},{11,1... | collective-permute-start | bytes 12296 | tf_op jit(solution)/shard_map/ppermute | solution.py:29
  104.4 54.9 %all-to-all-start.3 = ((f32[4,256,128]{2,1,0:T(8,128)}), f32[4,256,128]{2,1,0:T(8,128)S(1)}, u32[]{:S(2)}, u32[]{:S(2)}) async-start(f32[4,256,128]{2,1,0:T(8,128)} %bitcast.7), calls=%async_computation.3 | async-start | bytes 1048576 | tf_op jit(solution)/shard_map/all_to_all | solution.py:480
  108.3 3.8 %collective-permute-start.8 = (f32[4,1,1,768]{3,2,1,0:T(1,128)S(1)}, f32[4,1,1,768]{3,2,1,0:T(1,128)S(1)}, u32[]{:S(2)}, u32[]{:S(2)}) collective-permute-start(f32[4,1,1,768]{3,2,1,0:T(1,128)S(1)} %get-tuple-element.24), channel_id=1, source_target_pairs={{0,4},{4,0},{1,5},{5,1},{2,6},{6,2},{3,7},{7,3},{8,12},{12,8},{9,1... | collective-permute-start | bytes 36872 | tf_op jit(solution)/shard_map/ppermute | solution.py:26
  109.2 3.7 %collective-permute-start.9 = (f32[4,1,1,768]{3,2,1,0:T(1,128)S(1)}, f32[4,1,1,768]{3,2,1,0:T(1,128)S(1)}, u32[]{:S(2)}, u32[]{:S(2)}) collective-permute-start(f32[4,1,1,768]{3,2,1,0:T(1,128)S(1)} %get-tuple-element.25), channel_id=1, source_target_pairs={{4,0},{0,4},{5,1},{1,5},{6,2},{2,6},{7,3},{3,7},{12,8},{8,12},{13,... | collective-permute-start | bytes 36872 | tf_op jit(solution)/shard_map/ppermute | solution.py:29
  112.9 7.9 %collective-permute-start.10 = (f32[1,4,1,768]{3,2,1,0:T(1,128)S(1)}, f32[1,4,1,768]{3,2,1,0:T(1,128)S(1)}, u32[]{:S(2)}, u32[]{:S(2)}) collective-permute-start(f32[1,4,1,768]{3,2,1,0:T(1,128)S(1)} %get-tuple-element.22), channel_id=1, source_target_pairs={{0,8},{8,16},{16,24},{24,0},{1,9},{9,17},{17,25},{25,1},{2,10},{10... | collective-permute-start | bytes 36872 | tf_op jit(solution)/shard_map/ppermute | solution.py:26
  115.0 5.9 %collective-permute-start.11 = (f32[1,4,1,768]{3,2,1,0:T(1,128)S(1)}, f32[1,4,1,768]{3,2,1,0:T(1,128)S(1)}, u32[]{:S(2)}, u32[]{:S(2)}) collective-permute-start(f32[1,4,1,768]{3,2,1,0:T(1,128)S(1)} %get-tuple-element.23), channel_id=1, source_target_pairs={{8,0},{16,8},{24,16},{0,24},{9,1},{17,9},{25,17},{1,25},{10,2},{18... | collective-permute-start | bytes 36872 | tf_op jit(solution)/shard_map/ppermute | solution.py:29
  120.9 38.4 %copy-start.8 = (s32[4,2,4,128]{3,2,1,0:T(4,128)S(1)}, s32[4,2,4,128]{3,2,1,0:T(4,128)}, u32[]{:S(2)}) copy-start(s32[4,2,4,128]{3,2,1,0:T(4,128)} %sp.3) | copy-start | bytes 49156
  120.9 38.4 %copy-start.10 = (f32[2]{0:T(128)S(1)}, f32[2]{0:T(128)}, u32[]{:S(2)}) copy-start(f32[2]{0:T(128)} %tchg.3) | copy-start | bytes 28

commit v2 on v1

--- a/solution.py
+++ b/solution.py
@@ -1,3 +1,4 @@
+import functools
 import math
 
 import jax
@@ -18,17 +19,89 @@
 SM = pl.BlockSpec(memory_space=pltpu.SMEM)
 
 
-def padded(block, sides, widths):
-    for (axis, dim), width in zip(sides, widths):
-        count = lax.axis_size(axis)
-        forward = [(i, (i + 1) % count) for i in range(count)]
-        backward = [(target, source) for source, target in forward]
-        low = lax.ppermute(
-            lax.slice_in_dim(block, block.shape[dim] - width, None, axis=dim), axis, forward
+def exchange(mesh_sizes, spread, *refs):
+    gx, gy, gz = mesh_sizes
+    if spread:
+        pk, ch, ext, got, send, recv, a_send, a_recv, local = refs
+    else:
+        pk, ext, send, recv, local = refs
+    mx, my, mz = (lax.axis_index(a) for a in ("gx", "gy", "gz"))
+    nx, ny, _, lanes = pk.shape
+    dirs = [
+        (x, y, z) for x in (-1, 0, 1) for y in (-1, 0, 1) for z in (-1, 0, 1) if x or y or z
+    ]
+    peers = {(x % gx, y % gy, z % gz) for x, y, z in dirs}
+    if spread:
+        peers |= {(p, 0, 0) for p in range(1, gx)}
+
+    def at(x, y, z):
+        return {
+            "gx": lax.rem(mx + (x % gx), gx),
+            "gy": lax.rem(my + (y % gy), gy),
+            "gz": lax.rem(mz + (z % gz), gz),
+        }
+
+    barrier = pltpu.get_barrier_semaphore()
+    for peer in sorted(peers):
+        pl.semaphore_signal(
+            barrier, inc=1, device_id=at(*peer), device_id_type=pl.DeviceIdType.MESH
         )
-        high = lax.ppermute(lax.slice_in_dim(block, 0, width, axis=dim), axis, backward)
-        block = jnp.concatenate([low, block, high], axis=dim)
-    return block
+    pl.semaphore_wait(barrier, len(peers))
+
+    copies = []
+    if spread:
+        for p in range(1, gx):
+            target = at(p, 0, 0)
+            copies.append(
+                pltpu.make_async_remote_copy(
+                    src_ref=ch.at[target["gx"]],
+                    dst_ref=got.at[mx],
+                    send_sem=a_send.at[p - 1],
+                    recv_sem=a_recv.at[p - 1],
+                    device_id=target,
+                    device_id_type=pl.DeviceIdType.MESH,
+                )
+            )
+
+    def cut(step, count):
+        if step == 0:
+            return pl.ds(0, count), pl.ds(1, count)
+        if step > 0:
+            return pl.ds(count - 1, 1), pl.ds(0, 1)
+        return pl.ds(0, 1), pl.ds(count + 1, 1)
+
+    def cut_lanes(step):
+        if step == 0:
+            return pl.ds(0, lanes), pl.ds(128, lanes)
+        if step > 0:
+            return pl.ds(lanes - 128, 128), pl.ds(0, 128)
+        return pl.ds(0, 128), pl.ds(lanes + 128, 128)
+
+    for index, (x, y, z) in enumerate(dirs):
+        from_x, to_x = cut(x, nx)
+        from_y, to_y = cut(y, ny)
+        from_z, to_z = cut_lanes(z)
+        copies.append(
+            pltpu.make_async_remote_copy(
+                src_ref=pk.at[from_x, from_y, :, from_z],
+                dst_ref=ext.at[to_x, to_y, :, to_z],
+                send_sem=send.at[index],
+                recv_sem=recv.at[index],
+                device_id=at(x, y, z),
+                device_id_type=pl.DeviceIdType.MESH,
+            )
+        )
+    copies.append(
+        pltpu.make_async_copy(
+            pk, ext.at[pl.ds(1, nx), pl.ds(1, ny), :, pl.ds(128, lanes)], local.at[0]
+        )
+    )
+    if spread:
+        copies.append(pltpu.make_async_copy(ch.at[mx], got.at[mx], local.at[1]))
+    for copy in copies:
+        copy.start()
+    for copy in copies:
+        copy.wait()
 
 
 def split2(values):
@@ -53,10 +126,20 @@
     return mm(a[0], b[0], dims) + mm(a[0], b[1], dims) + mm(a[1], b[0], dims)
 
 
-def table(sp, ref):
+def mm6(a, b, dims=NN):
+    small = mm(a[0], b[2], dims) + mm(a[2], b[0], dims) + mm(a[1], b[1], dims)
+    return mm(a[0], b[0], dims) + (mm(a[0], b[1], dims) + (mm(a[1], b[0], dims) + small))
+
+
+def parts3(values):
+    return [part.astype(jnp.bfloat16) for part in split3(values)]
+
+
+def table(sp, ref, which):
     result = jnp.zeros(sp.shape, jnp.float32)
-    for kind in range(ref.shape[0]):
-        result = jnp.where(sp == kind, ref[kind], result)
+    kinds = ref.shape[0] // 4
+    for kind in range(kinds):
+        result = jnp.where(sp == kind, ref[which * kinds + kind], result)
     return result
 
 
@@ -80,29 +163,29 @@
     return jnp.concatenate(parts, axis=0)
 
 
-def spread_kernel(cnt, off, fr, sp, tden, tpair, temb, tchg, s_ref, pk_ref):
-    nx, ny, nz, _, slots = fr.shape
+def spread_kernel(cnt, off, fr, sp, tab, s_ref, pk_ref):
+    nx, ny, _, nz, slots = fr.shape
 
     def body(cx, carry):
         total = jnp.zeros((PPC * PPC, ny * nz * PPC), jnp.float32)
         for cy in range(ny):
             for cz in range(nz):
                 cell = cy * nz + cz
-                o = off[cx, cy, cz]
-                f = fr[cx, cy, cz]
+                o = jnp.concatenate([off[cx, cy, d, cz : cz + 1, :] for d in range(3)], axis=0)
+                f = jnp.concatenate([fr[cx, cy, d, cz : cz + 1, :] for d in range(3)], axis=0)
                 kind = sp[cx, cy, cz : cz + 1, :]
                 lane = lax.broadcasted_iota(jnp.int32, (1, slots), 1)
                 alive = (lane < cnt[(cx * ny + cy) * nz + cz]).astype(jnp.float32)
-                charge = table(kind, tchg) * alive
+                charge = table(kind, tab, 3) * alive
                 pos = (o.astype(jnp.float32) + 0.5 + f) / PPC
                 zero = jnp.zeros((1, slots), jnp.float32)
                 pk_ref[cx, cy, :, cz * slots : (cz + 1) * slots] = jnp.concatenate(
                     [
                         pos,
-                        table(kind, tden) * alive,
-                        table(kind, tpair) * alive,
+                        table(kind, tab, 0) * alive,
+                        table(kind, tab, 1) * alive,
                         alive,
-                        table(kind, temb),
+                        table(kind, tab, 2),
                         zero,
                     ],
                     axis=0,
@@ -126,9 +209,9 @@
     lax.fori_loop(0, nx, body, 0)
 
 
-def xmodes_kernel(direct, r_ref, qh, ql, h_ref):
+def xmodes_kernel(direct, r_ref, q_ref, h_ref):
     gx, ys, xs, lanes = r_ref.shape
-    q = (qh[...], ql[...])
+    q = split2(q_ref[...])
     for y in range(ys):
         data = r_ref[:, y].reshape(gx * xs, lanes)
         out = mm3(q, split2(data))
@@ -138,50 +221,64 @@
             h_ref[y] = out
 
 
-def xback_kernel(direct, h_ref, qh, ql, p_ref):
+def xback_kernel(direct, h_ref, q_ref, p_ref):
     gx, ys, xs, lanes = p_ref.shape
-    q = (qh[...], ql[...])
+    q = parts3(q_ref[...])
     for y in range(ys):
         data = h_ref[:, y].reshape(gx * xs, lanes) if direct else h_ref[y]
-        out = mm3(q, split2(data))
+        out = mm6(q, parts3(data))
         p_ref[:, y] = out.reshape(gx, xs, lanes)
 
 
-def plane_kernel(t_ref, wh, wl, kh, kl, green, o_ref):
+def plane_kernel(t_ref, z_ref, k_ref, green, o_ref):
     groups, gz, sub, lanes = t_ref.shape
     rows = groups * sub
     lz = green.shape[1]
-    ny = wh.shape[1] // lz
+    cut = lz // gz
+    ny = lanes // cut
+    q = z_ref[...]
+    blocks = []
+    for g in range(gz):
+        for c in range(ny):
+            pieces = [jnp.zeros((cut, lz), jnp.float32)] * ny
+            pieces[c] = q[g * cut : (g + 1) * cut]
+            blocks.append(jnp.concatenate(pieces, axis=1))
+    w = parts3(jnp.concatenate(blocks, axis=0))
+    k = parts3(k_ref[...])
     data = jnp.concatenate([t_ref[:, g].reshape(rows, lanes) for g in range(gz)], axis=1)
-    u = mm3(split2(data), (wh[...], wl[...]))
+    u = mm3(split2(data), w)
     u = jnp.concatenate([u[:, c * lz : (c + 1) * lz] for c in range(ny)], axis=0)
-    k = (kh[...], kl[...])
     v = mm3(k, split2(u)) * green[...]
-    u = mm3(k, split2(v))
+    u = mm6(k, parts3(v))
     u = jnp.concatenate([u[c * rows : (c + 1) * rows] for c in range(ny)], axis=1)
-    out = mm3(split2(u), (wh[...], wl[...]), NT)
+    out = mm6(parts3(u), w, NT)
     for g in range(gz):
         o_ref[:, g] = out[:, g * lanes : (g + 1) * lanes].reshape(groups, sub, lanes)
 
 
-def sample_kernel(cnt, off, fr, sp, tchg, phi_ref, eam, out_ref):
-    nx, ny, nz, _, slots = fr.shape
-
-    def body(cx, carry):
+def rest_of(low, right):
+    top = jnp.concatenate([low, jnp.zeros_like(low)], axis=1)
+    return jnp.concatenate([top, right], axis=0)
+
+
+def sample_kernel(cnt, off, fr, sp, tab, phi_ref, eam_a, eam_b, out_ref):
+    nx, ny, _, nz, slots = fr.shape
+
+    def body(cx, carry, eam, first):
         phi = phi_ref[:, pl.ds(pl.multiple_of(cx * PPC, PPC), PPC), :].reshape(
             PPC * PPC, ny * nz * PPC
         )
-        ph, pw = split2(phi)
+        ph, pw, pl3 = parts3(phi)
         both = jnp.concatenate([ph, pw], axis=1)
         for cy in range(ny):
             for cz in range(nz):
                 cell = cy * nz + cz
-                o = off[cx, cy, cz]
-                f = fr[cx, cy, cz]
+                o = jnp.concatenate([off[cx, cy, d, cz : cz + 1, :] for d in range(3)], axis=0)
+                f = jnp.concatenate([fr[cx, cy, d, cz : cz + 1, :] for d in range(3)], axis=0)
                 kind = sp[cx, cy, cz : cz + 1, :]
                 lane = lax.broadcasted_iota(jnp.int32, (1, slots), 1)
                 alive = (lane < cnt[(cx * ny + cy) * nz + cz]).astype(jnp.float32)
-                charge = table(kind, tchg) * alive
+                charge = table(kind, tab, 3) * alive
                 wx, sx = weights_of(o[0:1], f[0:1])
                 wy, sy = weights_of(o[1:2], f[1:2])
                 wz, sz = weights_of(o[2:3], f[2:3])
@@ -189,8 +286,9 @@
                 sh = placed(sz, cell, ny * nz).astype(jnp.bfloat16)
                 right = jnp.concatenate([zh, sh], axis=1)
                 g = mm(both, jnp.concatenate([right, right], axis=0))
-                gw = g[:, :slots] + mm(ph, zw)
-                gs = g[:, slots:]
+                more = mm(jnp.concatenate([ph, pl3], axis=1), rest_of(zw, right))
+                gw = g[:, :slots] + more[:, :slots]
+                gs = g[:, slots:] + more[:, slots:]
                 fx = jnp.zeros((PPC, slots), jnp.float32)
                 fy = jnp.zeros((PPC, slots), jnp.float32)
                 fz = jnp.zeros((PPC, slots), jnp.float32)
@@ -208,10 +306,14 @@
                     ],
                     axis=0,
                 )
-                out_ref[cx, cy, cz] = (eam[cx, cy, cz] - COUPLING * charge * field) * alive
+                out = (eam[cx - first, cy, cz] - COUPLING * charge * field) * alive
+                for d in range(3):
+                    out_ref[cx, cy, d, cz : cz + 1, :] = out[d : d + 1]
         return carry
 
-    lax.fori_loop(0, nx, body, 0)
+    half = eam_a.shape[0]
+    lax.fori_loop(0, half, lambda cx, c: body(cx, c, eam_a, 0), 0)
+    lax.fori_loop(half, nx, lambda cx, c: body(cx, c, eam_b, half), 0)
 
 
 def centred(ext, ex, ey, first_z, lanes, dims):
@@ -288,7 +390,11 @@
     return rows.T[:, :KF].astype(jnp.bfloat16)
 
 
-def force_kernel(ext, slope, f_ref, out_ref, rows_ref, acc, mine):
+def force_kernel(first, *refs):
+    if first == 0:
+        ext, slope, f_ref, out_ref, rows_ref, acc, mine = refs
+    else:
+        ext, rows_ref, f_ref, out_ref, acc, mine = refs
     ex_n, ey_n, _, lanes = ext.shape
     nx, ny = ex_n - 2, ey_n - 2
     slots = 128
@@ -306,7 +412,8 @@
         rows_ref[index] = jnp.concatenate([c * q, c, rho, t, jnp.zeros((2, lanes), jnp.float32)], 0)
         return carry
 
-    lax.fori_loop(0, ex_n * ey_n, build, 0)
+    if first == 0:
+        lax.fori_loop(0, ex_n * ey_n, build, 0)
 
     def cell(index, carry):
         ix = index // (ny * nz)
@@ -342,10 +449,11 @@
                         acc[a, at] += sums[a]
         total = [jnp.sum(acc[a].T, axis=0, keepdims=True) for a in range(4)]
         q = centred(own[0:3], ix + 1, iy + 1, iz + 1, slots, dims)
-        out_ref[ix, iy, iz] = own[3:4] * (jnp.concatenate(total[:3], axis=0) - q * total[3])
+        out_ref[ix - first, iy, iz] = own[3:4] * (jnp.concatenate(total[:3], axis=0) - q * total[3])
         return carry
 
-    lax.fori_loop(0, nx * ny * nz, cell, 0)
+    begin = first * ny * nz
+    lax.fori_loop(begin, begin + out_ref.shape[0] * ny * nz, cell, 0)
 
 
 def hartley(length):
@@ -354,13 +462,7 @@
     return (np.cos(phase) + np.sin(phase)) / np.sqrt(length)
 
 
-def halves(values):
-    high = values.astype(np.float32).astype(jnp.bfloat16)
-    low = (values - high.astype(np.float64)).astype(np.float32).astype(jnp.bfloat16)
-    return jnp.asarray(high), jnp.asarray(low)
-
-
-def call(kernel, out_shape, args, scalars=(), scratch=(), flops=1000000):
+def call(kernel, out_shape, args, scalars=(), scratch=(), flops=1000000, collective=None):
     specs = [SM if i in scalars else VM for i in range(len(args))]
     outs = jax.tree.map(lambda _: VM, out_shape)
     return pl.pallas_call(
@@ -369,7 +471,11 @@
         in_specs=specs,
         out_specs=outs,
         scratch_shapes=list(scratch),
-        compiler_params=pltpu.CompilerParams(vmem_limit_bytes=48 * 1024 * 1024),
+        compiler_params=pltpu.CompilerParams(
+            vmem_limit_bytes=48 * 1024 * 1024,
+            collective_id=collective,
+            has_side_effects=collective is not None,
+        ),
         cost_estimate=pl.CostEstimate(flops=flops, bytes_accessed=2000000, transcendentals=0),
     )(*args)
 
@@ -388,27 +494,36 @@
     counts = cell_counts.reshape(-1)
 
     sds = jax.ShapeDtypeStruct
+    tables = jnp.concatenate([t_den, t_pair, t_emb, t_chg])
+    offs = grid_offset.transpose(0, 1, 3, 2, 4)
+    fracs = fraction.transpose(0, 1, 3, 2, 4)
+    atoms = (counts, offs, fracs, species, tables)
     charge, packed = call(
         spread_kernel,
         (sds((PPC, xs, lanes), f32), sds((nx, ny, 8, nz * slots), f32)),
-        (counts, grid_offset, fraction, species, t_den, t_pair, t_emb, t_chg),
-        scalars=(0, 4, 5, 6, 7),
-    )
-    sides = (("gz", 3), ("gy", 1), ("gx", 0))
-    ext = padded(packed, sides, (slots, 1, 1))
-
-    qh, ql = halves(hartley(lx))
-    zmat = hartley(lz)
-    cut = nz * PPC
-    wide = np.zeros((gz, ny, cut, ny, lz))
-    for c in range(ny):
-        wide[:, c, :, c, :] = zmat.reshape(gz, cut, lz)
-    wh, wl = halves(wide.reshape(gz * lanes, ny * lz))
+        atoms,
+        scalars=(0, 4),
+    )
+    dma = pltpu.SemaphoreType.DMA
+    sizes = (gx, gy, gz)
+    ext, got = call(
+        functools.partial(exchange, sizes, True),
+        (
+            sds((nx + 2, ny + 2, 8, (nz + 2) * slots), f32),
+            sds((gx, ys * xs, lanes), f32),
+        ),
+        (packed, charge.reshape(gx, ys * xs, lanes)),
+        scratch=(dma((26,)), dma((26,)), dma((gx - 1,)), dma((gx - 1,)), dma((2,))),
+        collective=0,
+    )
+
+    q_x = jnp.asarray(hartley(lx).astype(np.float32))
+    q_z = q_x if lx == lz else jnp.asarray(hartley(lz).astype(np.float32))
     order = (
         np.arange(ly).reshape(gy, ny, gx, ys).transpose(1, 2, 0, 3).reshape(-1)
     )
     kron = np.kron(hartley(ly)[np.ix_(order, order)], np.eye(modes))
-    kh, kl = halves(kron)
+    q_y = jnp.asarray(kron.astype(np.float32))
 
     def wave(index, length):
         return np.minimum(index, length - index) * (2.0 * math.pi / length)
@@ -431,14 +546,12 @@
     )
 
     direct = modes % 8 == 0
-    got = lax.all_to_all(charge.reshape(gx, ys * xs, lanes), "gx", 0, 0, tiled=True)
     got = got.reshape(gx, ys, xs, lanes)
-    import functools
-
     mid = sds((n_dev, ys, modes, lanes) if direct else (ys, lx, lanes), f32)
-    modal = call(functools.partial(xmodes_kernel, direct), mid, (got, qh, ql))
+    modal = call(functools.partial(xmodes_kernel, direct), mid, (got, q_x))
     if not direct:
         modal = modal.reshape(ys, n_dev, modes, lanes).transpose(1, 0, 2, 3)
+    ext, modal = lax.optimization_barrier((ext, modal))
     modal = lax.all_to_all(modal.reshape(n_dev, ys * modes, lanes), every, 0, 0, tiled=True)
 
     density, slope, feats = call(
@@ -452,39 +565,57 @@
         scratch=(pltpu.VMEM((slots, slots), f32),),
         flops=400000000,
     )
-    ext_slope = padded(slope, sides, (slots, 1, 1))
+    green, slope = lax.optimization_barrier((green, slope))
 
     planes = call(
         plane_kernel,
         sds((gx * gy, gz, ys * modes, lanes), f32),
-        (modal.reshape(gx * gy, gz, ys * modes, lanes), wh, wl, kh, kl, green),
-    )
+        (modal.reshape(gx * gy, gz, ys * modes, lanes), q_z, q_y, green),
+    )
+    planes, slope = lax.optimization_barrier((planes, slope))
     back = lax.all_to_all(planes.reshape(n_dev, ys * modes, lanes), every, 0, 0, tiled=True)
+    ext_slope = call(
+        functools.partial(exchange, sizes, False),
+        sds((nx + 2, ny + 2, 1, (nz + 2) * slots), f32),
+        (slope,),
+        scratch=(dma((26,)), dma((26,)), dma((1,))),
+        collective=1,
+    )
+    half = max(nx // 2, 1)
+    scratch = (pltpu.VMEM((4, slots, slots), f32), pltpu.VMEM((2, slots, slots), f32))
+    eam_a, rows = call(
+        functools.partial(force_kernel, 0),
+        (
+            sds((half, ny, nz, 3, slots), f32),
+            sds(((nx + 2) * (ny + 2), 8, (nz + 2) * slots), f32),
+        ),
+        (ext, ext_slope, feats),
+        scratch=scratch,
+        flops=400000000,
+    )
+    q_back, rows = lax.optimization_barrier((q_x, rows))
     back = back.reshape(n_dev, ys, modes, lanes)
     if not direct:
         back = back.transpose(1, 0, 2, 3).reshape(ys, lx, lanes)
     lines = call(
-        functools.partial(xback_kernel, direct), sds((gx, ys, xs, lanes), f32), (back, qh, ql)
-    )
-    eam = call(
-        force_kernel,
-        sds((nx, ny, nz, 3, slots), f32),
-        (ext, ext_slope, feats),
-        scratch=(
-            pltpu.VMEM(((nx + 2) * (ny + 2), 8, (nz + 2) * slots), f32),
-            pltpu.VMEM((4, slots, slots), f32),
-            pltpu.VMEM((2, slots, slots), f32),
-        ),
-        flops=800000000,
-    )
+        functools.partial(xback_kernel, direct), sds((gx, ys, xs, lanes), f32), (back, q_back)
+    )
+    lines, rows = lax.optimization_barrier((lines, rows))
     phi = lax.all_to_all(lines.reshape(gx, ys * xs, lanes), "gx", 0, 0, tiled=True)
+    eam_b = call(
+        functools.partial(force_kernel, half),
+        sds((nx - half, ny, nz, 3, slots), f32),
+        (ext, rows, feats),
+        scratch=scratch,
+        flops=400000000,
+    )
     forces = call(
         sample_kernel,
-        sds((nx, ny, nz, 3, slots), f32),
-        (counts, grid_offset, fraction, species, t_chg, phi.reshape(PPC, xs, lanes), eam),
+        sds((nx, ny, 3, nz, slots), f32),
+        atoms + (phi.reshape(PPC, xs, lanes), eam_a, eam_b),
         scalars=(0, 4),
     )
-    return (forces, density)
+    return (forces.transpose(0, 1, 3, 2, 4), density)
 
 
 def solution(mesh):

time: 164 us -> 136 us (0.83)
  Pallas kernels: 72.2 us -> 113 us
  waiting for transfers between devices: 28.7 us -> 0.01 us
  blocking collectives: 20.6 us -> 0 us
  starting transfers between devices: 25.7 us -> 15.4 us
  local copies, waits for them, and re-layouts: 12.4 us -> 5.28 us
    pallas_call x7 -> x10, Pallas kernels: 72.2 us -> 113 us  [call(): pl.pallas_call(kernel, out_shape=out_shape, in_specs=specs, out_specs=out...]
    ppermute x12 -> x0, waiting for transfers between devices: 22.7 us -> none  [the longest x6 18.6 us: padded(): lax.ppermute(lax.slice_in_dim(block, block.shape[dim] - width, None, axis...]
    all_to_all x1 -> x0, blocking collectives: 20.6 us -> none  [on_device(): lax.all_to_all(charge.reshape(gx, ys * xs, lanes), 'gx', 0, 0, tiled=True)]
    ppermute x12 -> x0, starting transfers between devices: 15.2 us -> none  [the longest x6 8.3 us: padded(): lax.ppermute(lax.slice_in_dim(block, 0, width, axis=dim), axis, backward)]
    all_to_all x1, waiting for transfers between devices: 6.01 us -> 0.01 us  [on_device(): lax.all_to_all(modal.reshape(n_dev, ys * modes, lanes), every, 0, 0, tile...]
    unnamed x41 -> x24, local copies, waits for them, and re-layouts: 8.64 us -> 4.51 us
    all_to_all x1, starting transfers between devices: 2.98 us -> 5.83 us  [on_device(): lax.all_to_all(planes.reshape(n_dev, ys * modes, lanes), every, 0, 0, til...]
    all_to_all x1, starting transfers between devices: 3.71 us -> 5.55 us  [on_device(): lax.all_to_all(modal.reshape(n_dev, ys * modes, lanes), every, 0, 0, tile...]
  transfers between devices with their start and end apart: 15 -> 3, of which waited for: 9 -> 0; matrix products, arithmetic and copies ran while one was open for 5% -> 0% of each run, Pallas kernels for 40% -> 56%
where the time goes in v2:
time: 136 us; the launch traced here: 135 us
  Pallas kernels  113 us (83%)
  starting transfers between devices  15.4 us (11%)
  local copies, waits for them, and re-layouts  5.28 us (4%)
    pallas_call x10, Pallas kernels, call(): pl.pallas_call(kernel, out_shape=out_shape, in_specs=specs, out_specs=out...  113 us
    all_to_all x1, starting transfers between devices, on_device(): lax.all_to_all(planes.reshape(n_dev, ys * modes, lanes), every, 0, 0, til...  5.83 us
    all_to_all x1, starting transfers between devices, on_device(): lax.all_to_all(modal.reshape(n_dev, ys * modes, lanes), every, 0, 0, tile...  5.55 us
    unnamed x24, local copies, waits for them, and re-layouts  4.51 us
    all_to_all x1, starting transfers between devices, on_device(): lax.all_to_all(lines.reshape(gx, ys * xs, lanes), 'gx', 0, 0, tiled=True)  4.03 us
  transfers between devices with their start and end apart: 3, of which 0 were waited for; matrix products, arithmetic and copies ran while one was open for 0% of the time, Pallas kernels for 56%

profile of v2, /device:TPU:0, one launch (start us, length us, event | category | flops | bytes accessed | tf_op | source)
XLA Modules:
  0.0 135.4 jit_solution(1704042547681323582)
XLA Ops:
  0.6 0.8 reshape.31.cnt
  1.4 0.8 pad_maximum_fusion.tab
  2.2 0.8 copy-done.3
  3.0 0.8 copy-done.5
  3.8 0.7 copy-done.7
  4.5 2.9 %shard_map.140 = (f32[16,64,128]{2,1,0:T(8,128)S(1)}, f32[4,2,8,512]{3,2,1,0:T(8,128)S(1)}) custom-call(s32[32]{0:T(128)S(1)} %reshape.31.cnt, s32[4,2,3,4,128]{4,3,2,1,0:T(4,128)S(1)} %bitcast.17, f32[4,2,3,4,128]{4,3,2,1,0:T(4,128)S(1)} %bitcast.19, s32[4,2,4,128]{3,2,1,0:T(4,128)S(1)} %copy-done.7, f32[8]{0:T(128)S(1)} %pad_maximum_fusion.tab), custom_call_target="tpu_custom_call" | custom-call | flops 1000000 | bytes 2000000 | tf_op jit(solution)/shard_map/pallas_call | solution.py:468
  7.4 21.8 %shard_map.141 = (f32[6,4,8,768]{3,2,1,0:T(8,128)S(1)}, f32[4,256,128]{2,1,0:T(8,128)S(1)}) custom-call(f32[4,2,8,512]{3,2,1,0:T(8,128)S(1)} %get-tuple-element.21.refs_0_, f32[4,256,128]{2,1,0:T(8,128)S(1)} %bitcast.15), custom_call_target="tpu_custom_call" | custom-call | flops 1000000 | bytes 2000000 | tf_op jit(solution)/shard_map/pallas_call | solution.py:468
  29.3 0.0 copy-start
  29.3 0.9 copy-done
  30.2 1.4 %shard_map.142 = f32[32,4,8,128]{3,2,1,0:T(8,128)} custom-call(f32[4,4,64,128]{3,2,1,0:T(8,128)S(1)} %bitcast.16, f32[256,256]{1,0:T(8,128)S(1)} %copy-done), custom_call_target="tpu_custom_call" | custom-call | flops 1000000 | bytes 2000000 | tf_op jit(solution)/shard_map/pallas_call | solution.py:468
  31.6 5.5 %all-to-all-start = ((f32[32,32,128]{2,1,0:T(8,128)}), f32[32,32,128]{2,1,0:T(8,128)S(1)}, u32[]{:S(2)}, u32[]{:S(2)}) async-start(f32[32,32,128]{2,1,0:T(8,128)} %bitcast.4), calls=%async_computation | async-start | bytes 1048576 | tf_op jit(solution)/shard_map/all_to_all | solution.py:555
  37.1 0.0 copy-start.1
  37.2 21.8 %shard_map.143 = (f32[4,2,4,128]{3,2,1,0:T(4,128)}, f32[4,2,1,512]{3,2,1,0:T(1,128)S(1)}, bf16[24,32,768]{2,1,0:T(8,128)(2,1)S(1)}) custom-call(f32[6,4,8,768]{3,2,1,0:T(8,128)S(1)} %get-tuple-element.26.ext.refs_0_), custom_call_target="tpu_custom_call" | custom-call | flops 400000000 | bytes 2000000 | tf_op jit(solution)/shard_map/pallas_call | solution.py:468
  59.0 0.0 copy-done.9
  59.0 0.0 copy-done.10
  59.0 0.0 copy-done.11
  59.0 0.2 fusion.green
  59.3 0.0 all-to-all-done
  59.3 0.0 copy-done.1
  59.3 0.0 copy-start.2
  59.3 1.2 copy-done.2
  60.5 5.2 %shard_map.144 = f32[8,4,32,128]{3,2,1,0:T(8,128)} custom-call(f32[8,4,32,128]{3,2,1,0:T(8,128)S(1)} %bitcast.14, f32[256,256]{1,0:T(8,128)S(1)} %copy-done.1, f32[512,512]{1,0:T(8,128)S(1)} %copy-done.2, f32[512,256]{1,0:T(8,128)S(1)} %fusion.green), custom_call_target="tpu_custom_call" | custom-call | flops 1000000 | bytes 2000000 | tf_op jit(solution)/shard_map/pallas_call | solution.py:468
  65.7 5.8 %all-to-all-start.1 = ((f32[32,32,128]{2,1,0:T(8,128)}), f32[32,32,128]{2,1,0:T(8,128)S(1)}, u32[]{:S(2)}, u32[]{:S(2)}) async-start(f32[32,32,128]{2,1,0:T(8,128)} %bitcast.7), calls=%async_computation.1 | async-start | bytes 1048576 | tf_op jit(solution)/shard_map/all_to_all | solution.py:576
  71.6 15.4 %shard_map.145.refs_1_ = f32[6,4,1,768]{3,2,1,0:T(1,128)S(1)} custom-call(f32[4,2,1,512]{3,2,1,0:T(1,128)S(1)} %get-tuple-element.31.refs_0_), custom_call_target="tpu_custom_call" | custom-call | flops 1000000 | bytes 2000000 | tf_op jit(solution)/shard_map/pallas_call | solution.py:468
  87.0 19.5 %shard_map.146 = (f32[2,2,4,3,128]{4,3,2,1,0:T(4,128)S(1)}, f32[24,8,768]{2,1,0:T(8,128)S(1)}) custom-call(f32[6,4,8,768]{3,2,1,0:T(8,128)S(1)} %get-tuple-element.26.ext.refs_0_, f32[6,4,1,768]{3,2,1,0:T(1,128)S(1)} %shard_map.145.refs_1_, bf16[24,32,768]{2,1,0:T(8,128)(2,1)S(1)} %get-tuple-element.32.refs_2_), custom_call_target="tpu_custom_call" | custom-call | flops 400000000 | bytes 2000000 | tf_op jit(solution)/shard_map/pallas_call | solution.py:468
  106.5 0.0 all-to-all-done.1
  106.5 1.8 %shard_map.147 = f32[4,4,64,128]{3,2,1,0:T(8,128)} custom-call(f32[32,4,8,128]{3,2,1,0:T(8,128)S(1)} %bitcast.13, f32[256,256]{1,0:T(8,128)S(1)} %copy-done.1), custom_call_target="tpu_custom_call" | custom-call | flops 1000000 | bytes 2000000 | tf_op jit(solution)/shard_map/pallas_call | solution.py:468
  108.3 4.0 %all-to-all-start.2 = ((f32[4,256,128]{2,1,0:T(8,128)}), f32[4,256,128]{2,1,0:T(8,128)S(1)}, u32[]{:S(2)}, u32[]{:S(2)}) async-start(f32[4,256,128]{2,1,0:T(8,128)} %bitcast.9), calls=%async_computation.2 | async-start | bytes 1048576 | tf_op jit(solution)/shard_map/all_to_all | solution.py:604
  112.3 18.8 %shard_map.148.eam_b = f32[2,2,4,3,128]{4,3,2,1,0:T(4,128)S(1)} custom-call(f32[6,4,8,768]{3,2,1,0:T(8,128)S(1)} %get-tuple-element.26.ext.refs_0_, f32[24,8,768]{2,1,0:T(8,128)S(1)} %get-tuple-element.38.refs_1_, bf16[24,32,768]{2,1,0:T(8,128)(2,1)S(1)} %get-tuple-element.32.refs_2_), custom_call_target="tpu_custom_call" | custom-call | flops 400000000 | bytes 2000000 | tf_op jit(solution)/shard_map/pallas_call | solution.py:468
  131.2 0.0 all-to-all-done.2
  131.2 0.0 copy-done.4
  131.2 4.2 %shard_map.149 = f32[4,2,3,4,128]{4,3,2,1,0:T(4,128)} custom-call(s32[32]{0:T(128)S(1)} %reshape.31.cnt, s32[4,2,3,4,128]{4,3,2,1,0:T(4,128)S(1)} %bitcast.18, f32[4,2,3,4,128]{4,3,2,1,0:T(4,128)S(1)} %bitcast.20, s32[4,2,4,128]{3,2,1,0:T(4,128)S(1)} %copy-done.8, f32[8]{0:T(128)S(1)} %pad_maximum_fusion.tab, f32[16,64,128]{2,1,0:T(8,128)S(1)} %bitcast.12, ...), custom_call_target="tpu_custom_call" | custom-call | flops 1000000 | bytes 2000000 | tf_op jit(solution)/shard_map/pallas_call | solution.py:468
  (12 shorter events, 0.0 us)
Async XLA Ops:
  2.2 0.8 copy-start.3
  3.0 0.8 copy-start.5
  3.8 0.7 copy-start.7
  29.3 1.0 copy-start
  31.6 27.4 %copy-start.9 = (f32[512,1]{0,1:T(1,128)S(1)}, f32[512,1]{0,1:T(1,128)}, u32[]{:S(2)}) copy-start(f32[512,1]{0,1:T(1,128)} %constant.43.clone) | copy-start | bytes 6148
  31.6 27.4 %copy-start.10 = (s32[512,1]{0,1:T(1,128)S(1)}, s32[512,1]{0,1:T(1,128)}, u32[]{:S(2)}) copy-start(s32[512,1]{0,1:T(1,128)} %constant.42.clone) | copy-start | bytes 6148
  31.6 27.4 %copy-start.11 = (f32[256]{0:T(256)S(1)}, f32[256]{0:T(256)}, u32[]{:S(2)}) copy-start(f32[256]{0:T(256)} %constant.45) | copy-start | bytes 3076
  31.6 27.7 %all-to-all-start = ((f32[32,32,128]{2,1,0:T(8,128)}), f32[32,32,128]{2,1,0:T(8,128)S(1)}, u32[]{:S(2)}, u32[]{:S(2)}) async-start(f32[32,32,128]{2,1,0:T(8,128)} %bitcast.4), calls=%async_computation | async-start | bytes 1048576 | tf_op jit(solution)/shard_map/all_to_all | solution.py:555
  37.1 22.2 %copy-start.1 = (f32[256,256]{1,0:T(8,128)S(1)}, f32[256,256]{1,0:T(8,128)}, u32[]{:S(2)}) copy-start(f32[256,256]{1,0:T(8,128)} %constant.40.clone.q_ref.z_ref) | copy-start | bytes 786436
  59.3 1.2 copy-start.2
  65.7 40.8 %all-to-all-start.1 = ((f32[32,32,128]{2,1,0:T(8,128)}), f32[32,32,128]{2,1,0:T(8,128)S(1)}, u32[]{:S(2)}, u32[]{:S(2)}) async-start(f32[32,32,128]{2,1,0:T(8,128)} %bitcast.7), calls=%async_computation.1 | async-start | bytes 1048576 | tf_op jit(solution)/shard_map/all_to_all | solution.py:576
  108.3 22.9 %all-to-all-start.2 = ((f32[4,256,128]{2,1,0:T(8,128)}), f32[4,256,128]{2,1,0:T(8,128)S(1)}, u32[]{:S(2)}, u32[]{:S(2)}) async-start(f32[4,256,128]{2,1,0:T(8,128)} %bitcast.9), calls=%async_computation.2 | async-start | bytes 1048576 | tf_op jit(solution)/shard_map/all_to_all | solution.py:604
  112.3 18.9 %copy-start.4 = (s32[4,2,4,3,128]{4,2,3,1,0:T(4,128)S(1)}, s32[4,2,4,3,128]{4,2,3,1,0:T(4,128)}, u32[]{:S(2)}) copy-start(s32[4,2,4,3,128]{4,2,3,1,0:T(4,128)} %param.14) | copy-start | bytes 147460
  112.3 18.9 %copy-start.6 = (f32[4,2,4,3,128]{4,2,3,1,0:T(4,128)S(1)}, f32[4,2,4,3,128]{4,2,3,1,0:T(4,128)}, u32[]{:S(2)}) copy-start(f32[4,2,4,3,128]{4,2,3,1,0:T(4,128)} %param.15) | copy-start | bytes 147460
  112.3 18.9 %copy-start.8 = (s32[4,2,4,128]{3,2,1,0:T(4,128)S(1)}, s32[4,2,4,128]{3,2,1,0:T(4,128)}, u32[]{:S(2)}) copy-start(s32[4,2,4,128]{3,2,1,0:T(4,128)} %sp.3) | copy-start | bytes 49156

commit v3 on v2

--- a/solution.py
+++ b/solution.py
@@ -261,7 +261,7 @@
     return jnp.concatenate([top, right], axis=0)
 
 
-def sample_kernel(cnt, off, fr, sp, tab, phi_ref, eam_a, eam_b, out_ref):
+def sample_kernel(cnt, off, fr, sp, tab, phi_ref, eam_a, eam_b, eam_c, out_ref):
     nx, ny, _, nz, slots = fr.shape
 
     def body(cx, carry, eam, first):
@@ -313,7 +313,8 @@
 
     half = eam_a.shape[0]
     lax.fori_loop(0, half, lambda cx, c: body(cx, c, eam_a, 0), 0)
-    lax.fori_loop(half, nx, lambda cx, c: body(cx, c, eam_b, half), 0)
+    lax.fori_loop(half, 2 * half, lambda cx, c: body(cx, c, eam_b, half), 0)
+    lax.fori_loop(2 * half, nx, lambda cx, c: body(cx, c, eam_c, 2 * half), 0)
 
 
 def centred(ext, ex, ey, first_z, lanes, dims):
@@ -506,16 +507,15 @@
     )
     dma = pltpu.SemaphoreType.DMA
     sizes = (gx, gy, gz)
-    ext, got = call(
-        functools.partial(exchange, sizes, True),
-        (
-            sds((nx + 2, ny + 2, 8, (nz + 2) * slots), f32),
-            sds((gx, ys * xs, lanes), f32),
-        ),
-        (packed, charge.reshape(gx, ys * xs, lanes)),
-        scratch=(dma((26,)), dma((26,)), dma((gx - 1,)), dma((gx - 1,)), dma((2,))),
+    ext = call(
+        functools.partial(exchange, sizes, False),
+        sds((nx + 2, ny + 2, 8, (nz + 2) * slots), f32),
+        (packed,),
+        scratch=(dma((26,)), dma((26,)), dma((1,))),
         collective=0,
     )
+    charge, ext = lax.optimization_barrier((charge, ext))
+    got = lax.all_to_all(charge.reshape(gx, ys * xs, lanes), "gx", 0, 0, tiled=True)
 
     q_x = jnp.asarray(hartley(lx).astype(np.float32))
     q_z = q_x if lx == lz else jnp.asarray(hartley(lz).astype(np.float32))
@@ -545,15 +545,6 @@
         / jnp.where(anchor, 1.0, square),
     )
 
-    direct = modes % 8 == 0
-    got = got.reshape(gx, ys, xs, lanes)
-    mid = sds((n_dev, ys, modes, lanes) if direct else (ys, lx, lanes), f32)
-    modal = call(functools.partial(xmodes_kernel, direct), mid, (got, q_x))
-    if not direct:
-        modal = modal.reshape(ys, n_dev, modes, lanes).transpose(1, 0, 2, 3)
-    ext, modal = lax.optimization_barrier((ext, modal))
-    modal = lax.all_to_all(modal.reshape(n_dev, ys * modes, lanes), every, 0, 0, tiled=True)
-
     density, slope, feats = call(
         density_kernel,
         (
@@ -565,15 +556,7 @@
         scratch=(pltpu.VMEM((slots, slots), f32),),
         flops=400000000,
     )
-    green, slope = lax.optimization_barrier((green, slope))
-
-    planes = call(
-        plane_kernel,
-        sds((gx * gy, gz, ys * modes, lanes), f32),
-        (modal.reshape(gx * gy, gz, ys * modes, lanes), q_z, q_y, green),
-    )
-    planes, slope = lax.optimization_barrier((planes, slope))
-    back = lax.all_to_all(planes.reshape(n_dev, ys * modes, lanes), every, 0, 0, tiled=True)
+    q_first, slope = lax.optimization_barrier((q_x, slope))
     ext_slope = call(
         functools.partial(exchange, sizes, False),
         sds((nx + 2, ny + 2, 1, (nz + 2) * slots), f32),
@@ -581,7 +564,17 @@
         scratch=(dma((26,)), dma((26,)), dma((1,))),
         collective=1,
     )
-    half = max(nx // 2, 1)
+
+    direct = modes % 8 == 0
+    got = got.reshape(gx, ys, xs, lanes)
+    mid = sds((n_dev, ys, modes, lanes) if direct else (ys, lx, lanes), f32)
+    modal = call(functools.partial(xmodes_kernel, direct), mid, (got, q_first))
+    if not direct:
+        modal = modal.reshape(ys, n_dev, modes, lanes).transpose(1, 0, 2, 3)
+    ext_slope, modal = lax.optimization_barrier((ext_slope, modal))
+    modal = lax.all_to_all(modal.reshape(n_dev, ys * modes, lanes), every, 0, 0, tiled=True)
+
+    half = max(nx // 4, 1)
     scratch = (pltpu.VMEM((4, slots, slots), f32), pltpu.VMEM((2, slots, slots), f32))
     eam_a, rows = call(
         functools.partial(force_kernel, 0),
@@ -593,7 +586,23 @@
         scratch=scratch,
         flops=400000000,
     )
-    q_back, rows = lax.optimization_barrier((q_x, rows))
+    green, rows = lax.optimization_barrier((green, rows))
+
+    planes = call(
+        plane_kernel,
+        sds((gx * gy, gz, ys * modes, lanes), f32),
+        (modal.reshape(gx * gy, gz, ys * modes, lanes), q_z, q_y, green),
+    )
+    planes, rows = lax.optimization_barrier((planes, rows))
+    back = lax.all_to_all(planes.reshape(n_dev, ys * modes, lanes), every, 0, 0, tiled=True)
+    eam_b = call(
+        functools.partial(force_kernel, half),
+        sds((half, ny, nz, 3, slots), f32),
+        (ext, rows, feats),
+        scratch=scratch,
+        flops=200000000,
+    )
+    q_back, eam_b = lax.optimization_barrier((q_x, eam_b))
     back = back.reshape(n_dev, ys, modes, lanes)
     if not direct:
         back = back.transpose(1, 0, 2, 3).reshape(ys, lx, lanes)
@@ -602,9 +611,9 @@
     )
     lines, rows = lax.optimization_barrier((lines, rows))
     phi = lax.all_to_all(lines.reshape(gx, ys * xs, lanes), "gx", 0, 0, tiled=True)
-    eam_b = call(
-        functools.partial(force_kernel, half),
-        sds((nx - half, ny, nz, 3, slots), f32),
+    eam_c = call(
+        functools.partial(force_kernel, 2 * half),
+        sds((nx - 2 * half, ny, nz, 3, slots), f32),
         (ext, rows, feats),
         scratch=scratch,
         flops=400000000,
@@ -612,7 +621,7 @@
     forces = call(
         sample_kernel,
         sds((nx, ny, 3, nz, slots), f32),
-        atoms + (phi.reshape(PPC, xs, lanes), eam_a, eam_b),
+        atoms + (phi.reshape(PPC, xs, lanes), eam_a, eam_b, eam_c),
         scalars=(0, 4),
     )
     return (forces.transpose(0, 1, 3, 2, 4), density)

time: 136 us -> 133 us (0.978)
  Pallas kernels: 113 us -> 97.1 us
  waiting for transfers between devices: 0.01 us -> 10.6 us
  local copies, waits for them, and re-layouts: 5.28 us -> 7 us
    pallas_call x10 -> x11, Pallas kernels: 113 us -> 97.1 us  [call(): pl.pallas_call(kernel, out_shape=out_shape, in_specs=specs, out_specs=out...]
    all_to_all x1, waiting for transfers between devices: 0.01 us -> 6.18 us  [on_device(): lax.all_to_all(planes.reshape(n_dev, ys * modes, lanes), every, 0, 0, til...]
    all_to_all x1, waiting for transfers between devices: 0.01 us -> 4.4 us  [on_device(): lax.all_to_all(modal.reshape(n_dev, ys * modes, lanes), every, 0, 0, tile...]
    all_to_all x0 -> x1, starting transfers between devices: none -> 3.61 us  [on_device(): lax.all_to_all(charge.reshape(gx, ys * xs, lanes), 'gx', 0, 0, tiled=True)]
    all_to_all x1, starting transfers between devices: 5.83 us -> 2.97 us  [on_device(): lax.all_to_all(planes.reshape(n_dev, ys * modes, lanes), every, 0, 0, til...]
    unnamed x24 -> x28, local copies, waits for them, and re-layouts: 4.51 us -> 6.23 us
  transfers between devices with their start and end apart: 3 -> 4, of which waited for: 0 -> 2; matrix products, arithmetic and copies ran while one was open for 0% -> 1% of each run, Pallas kernels for 56% -> 52%
where the time goes in v3:
time: 133 us; the launch traced here: 132 us
  Pallas kernels  97.1 us (73%)
  starting transfers between devices  14.8 us (11%)
  waiting for transfers between devices  10.6 us (8%)
  local copies, waits for them, and re-layouts  7 us (5%)
  other arithmetic  1.85 us (1%)
    pallas_call x11, Pallas kernels, call(): pl.pallas_call(kernel, out_shape=out_shape, in_specs=specs, out_specs=out...  97.1 us
    unnamed x28, local copies, waits for them, and re-layouts  6.23 us
    all_to_all x1, waiting for transfers between devices, on_device(): lax.all_to_all(planes.reshape(n_dev, ys * modes, lanes), every, 0, 0, til...  6.18 us
    all_to_all x1, starting transfers between devices, on_device(): lax.all_to_all(modal.reshape(n_dev, ys * modes, lanes), every, 0, 0, tile...  4.52 us
    all_to_all x1, waiting for transfers between devices, on_device(): lax.all_to_all(modal.reshape(n_dev, ys * modes, lanes), every, 0, 0, tile...  4.4 us
    all_to_all x1, starting transfers between devices, on_device(): lax.all_to_all(lines.reshape(gx, ys * xs, lanes), 'gx', 0, 0, tiled=True)  3.65 us
    all_to_all x1, starting transfers between devices, on_device(): lax.all_to_all(charge.reshape(gx, ys * xs, lanes), 'gx', 0, 0, tiled=True)  3.61 us
    all_to_all x1, starting transfers between devices, on_device(): lax.all_to_all(planes.reshape(n_dev, ys * modes, lanes), every, 0, 0, til...  2.97 us
  transfers between devices with their start and end apart: 4, of which 2 were waited for; matrix products, arithmetic and copies ran while one was open for 1% of the time, Pallas kernels for 52%

profile of v3, /device:TPU:0, one launch (start us, length us, event | category | flops | bytes accessed | tf_op | source)
XLA Modules:
  0.0 132.2 jit_solution(17965271580026787803)
XLA Ops:
  0.6 0.8 reshape.31.cnt
  1.4 0.8 pad_maximum_fusion.tab
  2.2 0.8 copy-done.5
  3.0 0.8 copy-done.7
  3.8 0.7 copy-done.9
  4.5 3.7 %shard_map.140 = (f32[16,64,128]{2,1,0:T(8,128)}, f32[4,2,8,512]{3,2,1,0:T(8,128)S(1)}) custom-call(s32[32]{0:T(128)S(1)} %reshape.31.cnt, s32[4,2,3,4,128]{4,3,2,1,0:T(4,128)S(1)} %bitcast.18, f32[4,2,3,4,128]{4,3,2,1,0:T(4,128)S(1)} %bitcast.20, s32[4,2,4,128]{3,2,1,0:T(4,128)S(1)} %copy-done.9, f32[8]{0:T(128)S(1)} %pad_maximum_fusion.tab), custom_call_target="tpu_custom_call" | custom-call | flops 1000000 | bytes 2000000 | tf_op jit(solution)/shard_map/pallas_call | solution.py:469
  8.2 14.4 %shard_map.141.ext.refs_0_ = f32[6,4,8,768]{3,2,1,0:T(8,128)S(1)} custom-call(f32[4,2,8,512]{3,2,1,0:T(8,128)S(1)} %get-tuple-element.24.refs_0_), custom_call_target="tpu_custom_call" | custom-call | flops 1000000 | bytes 2000000 | tf_op jit(solution)/shard_map/pallas_call | solution.py:469
  22.7 0.0 copy-start
  22.7 3.6 %all-to-all-start = ((f32[4,256,128]{2,1,0:T(8,128)}), f32[4,256,128]{2,1,0:T(8,128)S(1)}, u32[]{:S(2)}, u32[]{:S(2)}) async-start(f32[4,256,128]{2,1,0:T(8,128)} %bitcast.2), calls=%async_computation | async-start | bytes 1048576 | tf_op jit(solution)/shard_map/all_to_all | solution.py:518
  26.3 21.8 %shard_map.142 = (f32[4,2,4,128]{3,2,1,0:T(4,128)}, f32[4,2,1,512]{3,2,1,0:T(1,128)S(1)}, bf16[24,32,768]{2,1,0:T(8,128)(2,1)S(1)}) custom-call(f32[6,4,8,768]{3,2,1,0:T(8,128)S(1)} %shard_map.141.ext.refs_0_), custom_call_target="tpu_custom_call" | custom-call | flops 400000000 | bytes 2000000 | tf_op jit(solution)/shard_map/pallas_call | solution.py:469
  48.1 8.0 %shard_map.143.refs_1_ = f32[6,4,1,768]{3,2,1,0:T(1,128)S(1)} custom-call(f32[4,2,1,512]{3,2,1,0:T(1,128)S(1)} %get-tuple-element.27.refs_0_), custom_call_target="tpu_custom_call" | custom-call | flops 1000000 | bytes 2000000 | tf_op jit(solution)/shard_map/pallas_call | solution.py:469
  56.2 0.0 copy-start.11
  56.2 0.0 copy-start.12
  56.2 0.0 copy-start.13
  56.2 1.4 %shard_map.144 = f32[32,4,8,128]{3,2,1,0:T(8,128)} custom-call(f32[4,4,64,128]{3,2,1,0:T(8,128)S(1)} %bitcast.13, f32[256,256]{1,0:T(8,128)S(1)} %copy-done), custom_call_target="tpu_custom_call" | custom-call | flops 1000000 | bytes 2000000 | tf_op jit(solution)/shard_map/pallas_call | solution.py:469
  57.6 4.5 %all-to-all-start.1 = ((f32[32,32,128]{2,1,0:T(8,128)}), f32[32,32,128]{2,1,0:T(8,128)S(1)}, u32[]{:S(2)}, u32[]{:S(2)}) async-start(f32[32,32,128]{2,1,0:T(8,128)} %bitcast.4), calls=%async_computation.1 | async-start | bytes 1048576 | tf_op jit(solution)/shard_map/all_to_all | solution.py:575
  62.2 1.1 fusion.green
  63.3 10.1 %shard_map.145 = (f32[1,2,4,3,128]{4,3,2,1,0:T(4,128)S(1)}, f32[24,8,768]{2,1,0:T(8,128)S(1)}) custom-call(f32[6,4,8,768]{3,2,1,0:T(8,128)S(1)} %shard_map.141.ext.refs_0_, f32[6,4,1,768]{3,2,1,0:T(1,128)S(1)} %shard_map.143.refs_1_, bf16[24,32,768]{2,1,0:T(8,128)(2,1)S(1)} %get-tuple-element.32.refs_2_), custom_call_target="tpu_custom_call" | custom-call | flops 400000000 | bytes 2000000 | tf_op jit(solution)/shard_map/pallas_call | solution.py:469
  73.4 4.4 %all-to-all-done.1 = f32[32,32,128]{2,1,0:T(8,128)S(1)} async-done(((f32[32,32,128]{2,1,0:T(8,128)}), f32[32,32,128]{2,1,0:T(8,128)S(1)}, u32[]{:S(2)}, u32[]{:S(2)}) %all-to-all-start.1) | async-done | bytes 524320 | tf_op jit(solution)/shard_map/all_to_all | solution.py:575
  77.8 1.0 copy-done.2
  78.8 1.2 copy-done.4
  80.0 4.4 %shard_map.146 = f32[8,4,32,128]{3,2,1,0:T(8,128)S(1)} custom-call(f32[8,4,32,128]{3,2,1,0:T(8,128)S(1)} %bitcast.16, f32[256,256]{1,0:T(8,128)S(1)} %copy-done, f32[512,512]{1,0:T(8,128)S(1)} %copy-done.4, f32[512,256]{1,0:T(8,128)S(1)} %copy-done.2), custom_call_target="tpu_custom_call" | custom-call | flops 1000000 | bytes 2000000 | tf_op jit(solution)/shard_map/pallas_call | solution.py:469
  84.4 0.8 copy-done.3
  85.2 3.0 %all-to-all-start.2 = ((f32[32,32,128]{2,1,0:T(8,128)}), f32[32,32,128]{2,1,0:T(8,128)S(1)}, u32[]{:S(2)}, u32[]{:S(2)}) async-start(f32[32,32,128]{2,1,0:T(8,128)} %bitcast.17), calls=%async_computation.2 | async-start | bytes 1048576 | tf_op jit(solution)/shard_map/all_to_all | solution.py:597
  88.2 9.4 %shard_map.147.eam_b = f32[1,2,4,3,128]{4,3,2,1,0:T(4,128)S(1)} custom-call(f32[6,4,8,768]{3,2,1,0:T(8,128)S(1)} %shard_map.141.ext.refs_0_, f32[24,8,768]{2,1,0:T(8,128)S(1)} %get-tuple-element.42.refs_1_, bf16[24,32,768]{2,1,0:T(8,128)(2,1)S(1)} %get-tuple-element.32.refs_2_), custom_call_target="tpu_custom_call" | custom-call | flops 200000000 | bytes 2000000 | tf_op jit(solution)/shard_map/pallas_call | solution.py:469
  97.7 6.2 %all-to-all-done.2 = f32[32,32,128]{2,1,0:T(8,128)S(1)} async-done(((f32[32,32,128]{2,1,0:T(8,128)}), f32[32,32,128]{2,1,0:T(8,128)S(1)}, u32[]{:S(2)}, u32[]{:S(2)}) %all-to-all-start.2) | async-done | bytes 524320 | tf_op jit(solution)/shard_map/all_to_all | solution.py:597
  103.8 1.0 shard_map.148
  104.8 0.8 copy-done.1
  105.6 3.6 %all-to-all-start.3 = ((f32[4,256,128]{2,1,0:T(8,128)}), f32[4,256,128]{2,1,0:T(8,128)S(1)}, u32[]{:S(2)}, u32[]{:S(2)}) async-start(f32[4,256,128]{2,1,0:T(8,128)} %bitcast.15), calls=%async_computation.3 | async-start | bytes 1048576 | tf_op jit(solution)/shard_map/all_to_all | solution.py:613
  109.3 0.0 copy-start.8
  109.3 18.8 %shard_map.149.eam_c = f32[2,2,4,3,128]{4,3,2,1,0:T(4,128)S(1)} custom-call(f32[6,4,8,768]{3,2,1,0:T(8,128)S(1)} %shard_map.141.ext.refs_0_, f32[24,8,768]{2,1,0:T(8,128)S(1)} %get-tuple-element.42.refs_1_, bf16[24,32,768]{2,1,0:T(8,128)(2,1)S(1)} %get-tuple-element.32.refs_2_), custom_call_target="tpu_custom_call" | custom-call | flops 400000000 | bytes 2000000 | tf_op jit(solution)/shard_map/pallas_call | solution.py:469
  128.2 4.0 %shard_map.150 = f32[4,2,3,4,128]{4,3,2,1,0:T(4,128)} custom-call(s32[32]{0:T(128)S(1)} %reshape.31.cnt, s32[4,2,3,4,128]{4,3,2,1,0:T(4,128)S(1)} %bitcast.19, f32[4,2,3,4,128]{4,3,2,1,0:T(4,128)S(1)} %bitcast.21, s32[4,2,4,128]{3,2,1,0:T(4,128)S(1)} %copy-done.10, f32[8]{0:T(128)S(1)} %pad_maximum_fusion.tab, f32[16,64,128]{2,1,0:T(8,128)S(1)} %bitcast.12, ...), custom_call_target="tpu_custom_call" | custom-call | flops 1000000 | bytes 2000000 | tf_op jit(solution)/shard_map/pallas_call | solution.py:469
  (19 shorter events, 0.1 us)
Async XLA Ops:
  2.2 0.8 copy-start.5
  3.0 0.8 copy-start.7
  3.8 0.7 copy-start.9
  22.7 33.5 %copy-start = (f32[256,256]{1,0:T(8,128)S(1)}, f32[256,256]{1,0:T(8,128)}, u32[]{:S(2)}) copy-start(f32[256,256]{1,0:T(8,128)} %constant.40.clone.q_ref.z_ref) | copy-start | bytes 786436
  22.7 33.5 %all-to-all-start = ((f32[4,256,128]{2,1,0:T(8,128)}), f32[4,256,128]{2,1,0:T(8,128)S(1)}, u32[]{:S(2)}, u32[]{:S(2)}) async-start(f32[4,256,128]{2,1,0:T(8,128)} %bitcast.2), calls=%async_computation | async-start | bytes 1048576 | tf_op jit(solution)/shard_map/all_to_all | solution.py:518
  56.2 6.0 %copy-start.11 = (f32[512,1]{0,1:T(1,128)S(1)}, f32[512,1]{0,1:T(1,128)}, u32[]{:S(2)}) copy-start(f32[512,1]{0,1:T(1,128)} %constant.43.clone) | copy-start | bytes 6148
  56.2 5.9 %copy-start.12 = (s32[512,1]{0,1:T(1,128)S(1)}, s32[512,1]{0,1:T(1,128)}, u32[]{:S(2)}) copy-start(s32[512,1]{0,1:T(1,128)} %constant.42.clone) | copy-start | bytes 6148
  56.2 6.0 %copy-start.13 = (f32[256]{0:T(256)S(1)}, f32[256]{0:T(256)}, u32[]{:S(2)}) copy-start(f32[256]{0:T(256)} %constant.45) | copy-start | bytes 3076
  57.6 20.1 %all-to-all-start.1 = ((f32[32,32,128]{2,1,0:T(8,128)}), f32[32,32,128]{2,1,0:T(8,128)S(1)}, u32[]{:S(2)}, u32[]{:S(2)}) async-start(f32[32,32,128]{2,1,0:T(8,128)} %bitcast.4), calls=%async_computation.1 | async-start | bytes 1048576 | tf_op jit(solution)/shard_map/all_to_all | solution.py:575
  77.8 1.0 copy-start.2
  78.8 1.2 copy-start.4
  84.4 0.8 copy-start.3
  85.2 18.6 %all-to-all-start.2 = ((f32[32,32,128]{2,1,0:T(8,128)}), f32[32,32,128]{2,1,0:T(8,128)S(1)}, u32[]{:S(2)}, u32[]{:S(2)}) async-start(f32[32,32,128]{2,1,0:T(8,128)} %bitcast.17), calls=%async_computation.2 | async-start | bytes 1048576 | tf_op jit(solution)/shard_map/all_to_all | solution.py:597
  104.8 0.8 copy-start.1
  105.6 22.6 %all-to-all-start.3 = ((f32[4,256,128]{2,1,0:T(8,128)}), f32[4,256,128]{2,1,0:T(8,128)S(1)}, u32[]{:S(2)}, u32[]{:S(2)}) async-start(f32[4,256,128]{2,1,0:T(8,128)} %bitcast.15), calls=%async_computation.3 | async-start | bytes 1048576 | tf_op jit(solution)/shard_map/all_to_all | solution.py:613
  109.3 18.9 %copy-start.6 = (s32[4,2,4,3,128]{4,2,3,1,0:T(4,128)S(1)}, s32[4,2,4,3,128]{4,2,3,1,0:T(4,128)}, u32[]{:S(2)}) copy-start(s32[4,2,4,3,128]{4,2,3,1,0:T(4,128)} %param.14) | copy-start | bytes 147460
  109.3 18.9 %copy-start.8 = (f32[4,2,4,3,128]{4,2,3,1,0:T(4,128)S(1)}, f32[4,2,4,3,128]{4,2,3,1,0:T(4,128)}, u32[]{:S(2)}) copy-start(f32[4,2,4,3,128]{4,2,3,1,0:T(4,128)} %param.15) | copy-start | bytes 147460
  109.3 18.9 %copy-start.10 = (s32[4,2,4,128]{3,2,1,0:T(4,128)S(1)}, s32[4,2,4,128]{3,2,1,0:T(4,128)}, u32[]{:S(2)}) copy-start(s32[4,2,4,128]{3,2,1,0:T(4,128)} %sp.3) | copy-start | bytes 49156
